TPU v7x, 768 devices: a whole 4x8x12 slice. The times are simulated.
768 devices in a mesh: dp: 12 (over x, z_lo), seq: 8 (over y), mp: 8 (over z_hi, core).
Axes of the slice: x: 4, y: 8, z: 12 (z_hi: 4, z_lo: 3; z = z_hi * 3 + z_lo), core: 2. Of those that a mesh axis runs over, the one named last changes fastest.
Arguments:
- inputs: bfloat16 [75264, 1024], P(('dp', 'seq', 'mp')), may hold values from -6 to 6
- grad_out: bfloat16 [75264, 1024], P(('dp', 'seq', 'mp')), may hold values from -6 to 6
- pad_mask: int32 [75264], P(('dp', 'seq', 'mp')), may hold values from 0 to 1, as said below
- hidden_pre: bfloat16 [75264, 4096], P(('dp', 'seq'), 'mp'), may hold values from -6 to 6
- w_in: bfloat16 [1024, 4096], P(None, 'mp'), may hold values from -0.1875 to 0.1875
- w_out: bfloat16 [4096, 1024], P('mp'), may hold values from -0.09375 to 0.09375
- ln_gain: float32 [1024], replicated, may hold values from 0.25 to 1.75
- ln_shift: float32 [1024], replicated, may hold values from -3 to 3
Outputs:
- grad_inputs: bfloat16 [75264, 1024], P(('dp', 'seq', 'mp'))
- grad_w_in: float32 [1024, 4096], P('seq', 'mp')
- grad_w_out: float32 [4096, 1024], P('mp', 'seq')
Inputs may be any that keep to these rules, and one draw needn't show every extreme that they name: `pad_mask`: each window is 196 consecutive tokens, 14 rows of 14 in row order; its image tokens are those in its first h rows and first w columns, h and w between 4 and 14; some windows are full and some are not in every draw.
All inputs are finite; a program needn't handle non-finite values.
Results may differ from a plain program's by a relative error of at most 0.02.
Values may be sent and summed in bfloat16 or wider, within the bound.
No kernel may reach another device: no remote copies, remote signals or barrier semaphores. Data moves between devices by JAX's collectives and lax.ppermute only.
A program may use at most 32 MiB of HBM per device.

v0:
```python
import jax
import jax.numpy as jnp
from jax import lax
from jax.sharding import PartitionSpec as P

EPSILON = 1e-06
ROOT_HALF = 0.7071067811865476
INV_ROOT_TAU = 0.3989422804014327


def side_by_side(arrays, axis, dim, along):
    both = jnp.concatenate(arrays, axis=along)
    whole, at, finished = (lax.all_gather(both, axis, axis=dim, tiled=True), 0, [])
    for a in arrays:
        finished.append(lax.slice_in_dim(whole, at, at + a.shape[along], axis=along))
        at += a.shape[along]
    return tuple(finished)


def cut_along(value, dim, count):
    lengths = value.shape
    pieces = value.reshape(*lengths[:dim], count, lengths[dim] // count, *lengths[dim + 1 :])
    return jnp.moveaxis(pieces, dim, 0)


def sum_at_owner(value, axis, dim):
    count = lax.axis_size(axis)
    pieces = lax.all_to_all(cut_along(value, dim, count), axis, 0, 0, tiled=True)
    return jnp.sum(pieces.astype(jnp.float32), axis=0)


def sum_packed(arrays, axis, dims):
    count = lax.axis_size(axis)
    pieces = [cut_along(a, dim, count) for a, dim in zip(arrays, dims)]
    lines = jnp.concatenate([b.reshape(count, -1) for b in pieces], axis=1)
    width = max(16, -(-lines.shape[1] // 1024) * 8)
    lines = jnp.pad(lines, ((0, 0), (0, width * 128 - lines.shape[1]))).reshape(-1, 128)
    line, at, finished = (lax.psum_scatter(lines, axis, tiled=True).reshape(-1), 0, [])
    for b in pieces:
        part = b[0]
        finished.append(line[at : at + part.size].reshape(part.shape))
        at += part.size
    return tuple(finished)


def sent_to_all(value, axis):
    copies = jnp.broadcast_to(value, (lax.axis_size(axis), *value.shape))
    return lax.all_to_all(copies, axis, split_axis=0, concat_axis=0, tiled=True)


def of_everyone(value, axis):
    return sent_to_all(value, axis).astype(jnp.float32).sum(axis=0)


def gelu_pair(hidden_pre):
    values = hidden_pre.astype(jnp.float32)
    normal_cdf = 0.5 * (1.0 + lax.erf(values * ROOT_HALF))
    normal_pdf = jnp.exp(-0.5 * values * values) * INV_ROOT_TAU
    return (values * normal_cdf, normal_cdf + values * normal_pdf)


def shards(inputs, grad_out, pad_mask, hidden_pre, w_in, w_out, ln_gain, ln_shift):
    own_rows = inputs.shape[0]
    values = inputs.astype(jnp.float32)
    row_mean = jnp.mean(values, axis=1, keepdims=True)
    centred = values - row_mean
    row_var = jnp.mean(centred * centred, axis=1, keepdims=True)
    inv_std = lax.rsqrt(row_var + EPSILON)
    x_hat = centred * inv_std
    normed = (x_hat * ln_gain + ln_shift).astype(jnp.bfloat16)
    masked = (grad_out.astype(jnp.float32) * pad_mask.astype(jnp.float32)[:, None]).astype(
        jnp.bfloat16
    )
    normed_all, masked_all = side_by_side((normed, masked), "mp", 0, 1)
    activation, slope = gelu_pair(hidden_pre)
    activation = activation.astype(jnp.bfloat16)
    d_act = jnp.dot(masked_all, w_out.T, preferred_element_type=jnp.float32)
    d_hidden = (d_act * slope).astype(jnp.bfloat16)
    term_out = jnp.dot(activation.T, masked_all, preferred_element_type=jnp.float32)
    term_in = jnp.dot(normed_all.T, d_hidden, preferred_element_type=jnp.float32)
    d_normed = sum_at_owner(
        jnp.dot(d_hidden, w_in.T, preferred_element_type=jnp.float32).astype(jnp.bfloat16), "mp", 0
    )
    d_hat = d_normed * ln_gain
    first_term = jnp.mean(d_hat, axis=1, keepdims=True)
    second_term = jnp.mean(d_hat * x_hat, axis=1, keepdims=True)
    grad_inputs = (
        masked.astype(jnp.float32) + inv_std * (d_hat - first_term - x_hat * second_term)
    ).astype(jnp.bfloat16)
    piece_in, piece_out = tuple(
        (
            part.astype(jnp.float32)
            for part in sum_packed(
                (term_in.astype(jnp.bfloat16), term_out.astype(jnp.bfloat16)), "seq", (0, 1)
            )
        )
    )
    piece_in, piece_out = (
        of_everyone(piece_in.astype(jnp.bfloat16), "dp").astype(jnp.float32),
        of_everyone(piece_out.astype(jnp.bfloat16), "dp").astype(jnp.float32),
    )
    token_total = own_rows * lax.axis_size("dp") * lax.axis_size("seq") * lax.axis_size("mp")
    scale = float(token_total) ** (-0.5)
    return (grad_inputs, piece_in * scale, piece_out * scale)


def solution(mesh):
    return jax.shard_map(
        shards,
        mesh=mesh,
        in_specs=(
            P(("dp", "seq", "mp"), None),
            P(("dp", "seq", "mp"), None),
            P(("dp", "seq", "mp")),
            P(("dp", "seq"), "mp"),
            P(None, "mp"),
            P("mp", None),
            P(),
            P(),
        ),
        out_specs=(P(("dp", "seq", "mp"), None), P("seq", "mp"), P("mp", "seq")),
        check_vma=False,
    )
```

profile of v0, /device:TPU:192, one launch (start us, length us, event | category | flops | bytes accessed | tf_op | source)
XLA Modules:
  0.0 245.6 jit_solution(175735020605552018)
XLA Ops:
  7.2 0.0 copy-start
  7.2 0.0 all-gather.3.cloned.1.call-start
  7.2 0.7 convert_element_type.53
  8.0 1.1 convert_reduce_fusion.3
  9.0 1.2 fusion.32
  10.2 1.3 fusion.26
  11.5 0.8 maximum_bitcast_fusion
  12.3 0.0 all-gather.3.cloned.1.call-update
  12.3 0.0 copy-start.6
  12.4 0.0 reduce-scatter.2.cloned.1.call-start
  12.4 71.4 %all-gather.3.cloned.1.call-done = bf16[8,98,2048]{2,1,0:T(8,128)(2,1)} async-done(((bf16[1,98,2048]{2,1,0:T(8,128)(2,1)}), bf16[8,98,2048]{2,1,0:T(8,128)(2,1)}) %all-gather.3.cloned.1.call-update) | async-done | bytes 3211280 | tf_op jit(solution)/shard_map/all_gather | solution.py:13
  83.8 3.6 %reshape.56 = bf16[784,2048]{1,0:T(8,128)(2,1)} reshape(bf16[8,98,2048]{2,1,0:T(8,128)(2,1)} %all-gather.3.cloned.1.call-done) | data formatting | bytes 6422528
  87.4 0.0 copy-done.6
  87.4 2.9 %fusion.16 = bf16[64,8,8,128]{3,1,2,0:T(8,128)(2,1)S(1)} fusion(bf16[784,2048]{1,0:T(8,128)(2,1)} %reshape.56, bf16[784,512]{1,0:T(8,128)(2,1)S(1)} %copy-done.6), kind=kOutput, calls=%fused_computation.25 | convolution fusion | flops 825016320 | bytes 3457024 | tf_op jit(solution)/shard_map/dot_general | solution.py:79
  90.3 0.0 copy-done.3
  90.3 0.0 copy-done.5
  90.3 1.5 fusion.7
  91.8 0.0 copy-start.7
  91.8 1.3 fusion.11
  93.1 0.0 copy-done.7
  93.1 1.3 copy.11
  94.4 1.5 reshape_reshape.3
  95.9 1.7 pad_maximum_fusion
  97.6 2.3 reshape.53
  99.9 0.0 reduce-scatter.2.cloned.1.call-update
  99.9 2.2 convolution_convert_fusion
  102.1 1.4 reshape.50
  103.5 7.0 %all-to-all-start = ((bf16[8,98,1024]{2,1,0:T(8,128)(2,1)}), bf16[8,98,1024]{2,1,0:T(8,128)(2,1)S(1)}, u32[]{:S(2)}, u32[]{:S(2)}) async-start(bf16[8,98,1024]{2,1,0:T(8,128)(2,1)} %reshape.50), calls=%async_computation | async-start | bytes 3407872 | tf_op jit(solution)/shard_map/all_to_all | solution.py:28
  110.5 35.2 %reduce-scatter.2.cloned.1.call-done = bf16[1024,128]{1,0:T(8,128)(2,1)} async-done(((bf16[8192,128]{1,0:T(8,128)(2,1)}), bf16[1024,128]{1,0:T(8,128)(2,1)}) %reduce-scatter.2.cloned.1.call-update) | async-done | bytes 262160 | tf_op jit(solution)/shard_map/reduce_scatter | solution.py:38
  145.6 1.0 fusion.34
  146.6 0.1 reshape.54
  146.7 18.6 %all-to-all-done = bf16[8,98,1024]{2,1,0:T(8,128)(2,1)S(1)} async-done(((bf16[8,98,1024]{2,1,0:T(8,128)(2,1)}), bf16[8,98,1024]{2,1,0:T(8,128)(2,1)S(1)}, u32[]{:S(2)}, u32[]{:S(2)}) %all-to-all-start) | async-done | bytes 1605664 | tf_op jit(solution)/shard_map/all_to_all | solution.py:28
  165.3 0.1 broadcast_in_dim.4
  165.5 37.3 %all_to_all.15 = bf16[12,128,512]{2,1,0:T(8,128)(2,1)} all-to-all(bf16[12,128,512]{2,1,0:T(8,128)(2,1)S(1)} %broadcast_in_dim.4), channel_id=1, replica_groups=mesh['dp'=12,'seq'=8,'mp'=8] {'dp'}, dimensions={0} | all-to-all | bytes 3145728 | tf_op jit(solution)/shard_map/all_to_all | solution.py:48
  202.8 1.4 broadcast_in_dim.5
  204.2 4.4 %all-to-all-start.2 = ((bf16[12,512,128]{2,1,0:T(8,128)(2,1)}), bf16[12,512,128]{2,1,0:T(8,128)(2,1)}, u32[]{:S(2)}, u32[]{:S(2)}) async-start(bf16[12,512,128]{2,1,0:T(8,128)(2,1)} %broadcast_in_dim.5), calls=%async_computation.3 | async-start | bytes 3145728 | tf_op jit(solution)/shard_map/all_to_all | solution.py:48
  208.6 0.0 copy-start.2
  208.6 0.0 copy-start.4
  208.6 0.0 copy-start.1
  208.6 0.3 convert_reduce_fusion
  208.9 0.6 copy-done.2
  209.5 0.2 multiply_reduce_fusion
  209.8 0.9 fusion.31
  210.7 0.2 convert_reduce_fusion.2
  210.9 0.7 broadcast_multiply_fusion.1
  211.6 24.7 %all-to-all-done.2 = bf16[12,512,128]{2,1,0:T(8,128)(2,1)} async-done(((bf16[12,512,128]{2,1,0:T(8,128)(2,1)}), bf16[12,512,128]{2,1,0:T(8,128)(2,1)}, u32[]{:S(2)}, u32[]{:S(2)}) %all-to-all-start.2) | async-done | bytes 1572896 | tf_op jit(solution)/shard_map/all_to_all | solution.py:48
  236.3 1.6 convert_reduce_fusion.1
  238.0 0.7 broadcast_multiply_fusion
  (9 shorter events, 0.0 us)
Async XLA Ops:
  7.2 92.7 %copy-start = (bf16[1024,512]{1,0:T(8,128)(2,1)S(1)}, bf16[1024,512]{1,0:T(8,128)(2,1)}, u32[]{:S(2)}) copy-start(bf16[1024,512]{1,0:T(8,128)(2,1)} %param.12) | copy-start | bytes 3145732
  7.2 76.6 %all-gather.3.cloned.1.call-start = ((), (), s32[]{:S(2)}) async-start(), calls=%async_computation.5 | async-start | bytes 3833856 | tf_op jit(solution)/shard_map/all_gather | solution.py:13
  12.3 75.1 %copy-start.6 = (bf16[784,512]{1,0:T(8,128)(2,1)S(1)}, bf16[784,512]{1,0:T(8,128)(2,1)}, u32[]{:S(2)}) copy-start(bf16[784,512]{1,0:T(8,128)(2,1)} %param.11) | copy-start | bytes 2408452
  12.4 133.3 %reduce-scatter.2.cloned.1.call-start = ((), (), s32[]{:S(2)}) async-start(), calls=%async_computation.4 | async-start | bytes 2359296 | tf_op jit(solution)/shard_map/reduce_scatter | solution.py:38
  87.4 2.9 %copy-start.3 = (bf16[784,2048]{1,0:T(8,128)(2,1)S(1)}, bf16[784,2048]{1,0:T(8,128)(2,1)}, u32[]{:S(2)}) copy-start(bf16[784,2048]{1,0:T(8,128)(2,1)} %reshape.56) | copy-start | bytes 9633796
  87.4 2.9 %copy-start.5 = (bf16[512,1024]{1,0:T(8,128)(2,1)S(1)}, bf16[512,1024]{1,0:T(8,128)(2,1)}, u32[]{:S(2)}) copy-start(bf16[512,1024]{1,0:T(8,128)(2,1)} %param.13) | copy-start | bytes 3145732
  91.8 1.3 copy-start.7
  103.5 61.8 %all-to-all-start = ((bf16[8,98,1024]{2,1,0:T(8,128)(2,1)}), bf16[8,98,1024]{2,1,0:T(8,128)(2,1)S(1)}, u32[]{:S(2)}, u32[]{:S(2)}) async-start(bf16[8,98,1024]{2,1,0:T(8,128)(2,1)} %reshape.50), calls=%async_computation | async-start | bytes 3407872 | tf_op jit(solution)/shard_map/all_to_all | solution.py:28
  204.2 32.2 %all-to-all-start.2 = ((bf16[12,512,128]{2,1,0:T(8,128)(2,1)}), bf16[12,512,128]{2,1,0:T(8,128)(2,1)}, u32[]{:S(2)}, u32[]{:S(2)}) async-start(bf16[12,512,128]{2,1,0:T(8,128)(2,1)} %broadcast_in_dim.5), calls=%async_computation.3 | async-start | bytes 3145728 | tf_op jit(solution)/shard_map/all_to_all | solution.py:48
  208.6 0.9 copy-start.2
  208.6 0.9 copy-start.4
  208.6 2.1 copy-start.1
Sparse Core Ops, SparseCore 0:
  12.5 71.2 all-gather.2
  100.0 45.5 reduce-scatter.1
where the time goes:
time: 246 us
  waiting for transfers between devices  150 us (61%)
  blocking collectives  37.3 us (15%)
  between operations  14.2 us (6%)
  local copies, waits for them, and re-layouts  13.4 us (5%)
  starting transfers between devices  11.5 us (5%)
  other arithmetic  11.5 us (5%)
  matrix products  7.78 us (3%)
    all_gather x1, waiting for transfers between devices, side_by_side(): lax.all_gather(both, axis, axis=dim, tiled=True)  71.4 us
    all_to_all x1, blocking collectives, sent_to_all(): return lax.all_to_all(copies, axis, split_axis=0, concat_axis=0, tiled=True)  37.3 us
    reduce_scatter x1, waiting for transfers between devices, sum_packed(): lax.psum_scatter(lines, axis, tiled=True).reshape(-1)  35.2 us
    all_to_all x1, waiting for transfers between devices, sent_to_all(): return lax.all_to_all(copies, axis, split_axis=0, concat_axis=0, tiled=True)  24.7 us
    all_to_all x1, waiting for transfers between devices, sum_at_owner(): lax.all_to_all(cut_along(value, dim, count), axis, 0, 0, tiled=True)  18.6 us
    all_to_all x1, starting transfers between devices, sum_at_owner(): lax.all_to_all(cut_along(value, dim, count), axis, 0, 0, tiled=True)  6.99 us
    unnamed x18, local copies, waits for them, and re-layouts  5.53 us
  transfers between devices with their start and end apart: 4, of which 4 were waited for; matrix products, arithmetic and copies ran while one was open for 3% of the time, Pallas kernels for 0%

commit v1 on v0

v1 whole, which is shorter than its diff:
```python
import jax
import jax.numpy as jnp
from jax import lax
from jax.experimental import pallas as pl
from jax.experimental.pallas import tpu as pltpu
from jax.sharding import Mesh, PartitionSpec as P


EPSILON = 1e-06
ROOT_HALF = 0.7071067811865476
INV_ROOT_TAU = 0.3989422804014327


BF = jnp.bfloat16
LIMIT = 40 * 1024 * 1024
F32 = jnp.float32


def shifted(value, axis, step):
    n = lax.axis_size(axis)
    return lax.ppermute(value, axis, [(i, (i + step) % n) for i in range(n)])


def gelu_pair(hidden_pre):
    values = hidden_pre.astype(F32)
    normal_cdf = 0.5 * (1.0 + lax.erf(values * ROOT_HALF))
    normal_pdf = jnp.exp(-0.5 * values * values) * INV_ROOT_TAU
    return (values * normal_cdf, normal_cdf + values * normal_pdf)


NT = (((1,), (1,)), ((), ()))
NN = (((1,), (0,)), ((), ()))


def dot(a, b, dims):
    return lax.dot_general(a, b, dims, preferred_element_type=F32)


def in_hbm(body, outs, scratch, fetched, smem=()):
    ni, no, ns = len(fetched), len(outs), len(smem)

    def whole(*refs):
        scalars, src, dst = refs[:ns], refs[ns : ns + ni], refs[ns + ni : ns + ni + no]
        in_sem, out_sem, *rest = refs[ns + ni + no :]
        held, made, extra = rest[:ni], rest[ni : ni + no], rest[ni + no :]
        gets = [pltpu.make_async_copy(src[k], held[k], in_sem.at[k]) for k in range(ni)]
        puts = [pltpu.make_async_copy(made[k], dst[k], out_sem.at[k]) for k in range(no)]
        for g in gets:
            g.start()
        body(scalars, gets, puts, held, made, *extra)
        for p in puts:
            p.wait()

    hbm = pl.BlockSpec(memory_space=pltpu.HBM)
    return pl.pallas_call(
        whole,
        out_shape=[pltpu.HBM(v.shape, v.dtype) for v in outs],
        in_specs=[pl.BlockSpec(memory_space=pltpu.SMEM)] * ns + [hbm] * ni,
        out_specs=[hbm] * no,
        scratch_shapes=[
            pltpu.SemaphoreType.DMA((ni,)),
            pltpu.SemaphoreType.DMA((no,)),
            *[pltpu.VMEM(v.shape, v.dtype) for v in (*fetched, *outs)],
            *scratch,
        ],
        compiler_params=pltpu.CompilerParams(vmem_limit_bytes=LIMIT),
    )(*smem, *(pltpu.with_memory_space_constraint(v, pltpu.HBM) for v in fetched))


def shaped(shape, dtype=BF):
    return jax.ShapeDtypeStruct(shape, dtype)


def stack_rows(refs, spots, buf, rows, padded):
    d = buf.shape[1]
    for k, (which, lane) in enumerate(spots):
        at = k * padded
        buf[at + padded - 16 : at + padded, :] = jnp.zeros((16, d), buf.dtype)
        buf[at : at + rows, :] = refs[which][:, lane * d : (lane + 1) * d]


def norm_and_mask(inputs, grad_out, pad_mask, ln_gain, ln_shift):
    rows, d = inputs.shape

    def body(x_ref, g_ref, m_ref, gain_ref, shift_ref, out_ref):
        values = x_ref[...].astype(F32)
        centred = values - jnp.mean(values, axis=1, keepdims=True)
        row_var = jnp.mean(centred * centred, axis=1, keepdims=True)
        x_hat = centred * lax.rsqrt(row_var + EPSILON)
        out_ref[:, :d] = (g_ref[...].astype(F32) * m_ref[...].astype(F32)).astype(BF)
        out_ref[:, d:] = (x_hat * gain_ref[...] + shift_ref[...]).astype(BF)

    vmem = pl.BlockSpec(memory_space=pltpu.VMEM)
    return pl.pallas_call(
        body,
        out_shape=shaped((rows, 2 * d)),
        in_specs=[vmem] * 5,
        out_specs=vmem,
    )(inputs, grad_out, pad_mask[:, None], ln_gain[None], ln_shift[None])


def weight_terms(arrays, m_spots, n_spots, act_t, w_out, slope, x_idx, nx, ny, rows, padded):
    na, n = len(arrays), len(m_spots)
    ff, d = w_out.shape
    total, p, q = n * padded, ff // nx, d // ny

    def body(scalars, gets, puts, held, made, m_buf, n_buf, slabs):
        act_ref, wo_ref, slope_ref = held[na:]
        for g in gets[:na]:
            g.wait()
        stack_rows(held, m_spots, m_buf, rows, padded)
        stack_rows(held, n_spots, n_buf, rows, padded)
        m = m_buf[...]
        for g in gets[na:]:
            g.wait()
        dh = (dot(m, wo_ref[...], NT) * slope_ref[...]).astype(BF)
        made[nx][...] = dh
        puts[nx].start()
        t_out = dot(act_ref[...], m, NN).astype(BF)
        t_in = dot(dh.T, n_buf[...], NN).astype(BF)
        for k in range(nx):
            for j in range(ny):
                rk, cj = slice(k * p, (k + 1) * p), slice(j * q, (j + 1) * q)
                slabs[k, j, :q, :] = t_in[rk, cj].T
                slabs[k, j, q:, :] = t_out[rk, cj]
        for k in range(nx):
            made[k][...] = slabs[(scalars[0][0] + k) % nx]
            puts[k].start()

    assert p == q
    return in_hbm(
        body,
        [shaped((ny, 2 * q, p))] * nx + [shaped((total, ff))],
        [pltpu.VMEM((total, d), BF), pltpu.VMEM((total, d), BF), pltpu.VMEM((nx, ny, 2 * q, p), BF)],
        (*arrays, act_t, w_out, slope),
        (x_idx,),
    )


def input_grad(d_hidden, w_in, rows, padded):
    total, _ = d_hidden.shape
    d = w_in.shape[0]
    nh = total // padded // 2

    def body(_, gets, puts, held, made):
        for g in gets:
            g.wait()
        r = dot(held[0][...], held[1][...], NT).astype(BF)
        for half in (1, 0):
            for k in range(nh):
                at = (2 * k + half) * padded
                made[half][:, k * d : (k + 1) * d] = r[at : at + rows]
            puts[half].start()

    return in_hbm(body, [shaped((rows, nh * d))] * 2, [], (d_hidden, w_in))


def shards(inputs, grad_out, pad_mask, hidden_pre, w_in, w_out, ln_gain, ln_shift):
    rows, d = inputs.shape
    nh, nc = lax.axis_size("zh"), lax.axis_size("c")
    nx, ny, nz = lax.axis_size("x"), lax.axis_size("y"), lax.axis_size("zl")
    n = nh * nc
    ff = hidden_pre.shape[1]
    padded = -(-rows // 16) * 16
    both_own = norm_and_mask(inputs, grad_out, pad_mask, ln_gain, ln_shift)
    both3 = shifted(both_own, "zh", 1)
    both1 = shifted(both_own, "zh", -1)

    zh, c = lax.axis_index("zh"), lax.axis_index("c")
    h = hidden_pre.reshape(nh, nc, rows, ff)
    h = lax.dynamic_slice_in_dim(jnp.concatenate([h, h[:-1]], axis=0), zh, nh, axis=0)
    h = lax.dynamic_slice_in_dim(jnp.concatenate([h, h[:, :-1]], axis=1), c, nc, axis=1)
    h = jnp.pad(h.reshape(n, rows, ff), ((0, 0), (0, padded - rows), (0, 0)))
    activation, slope = gelu_pair(h.reshape(n * padded, ff))
    act_t = activation.astype(BF).T

    m2 = shifted(both3[:, :d], "zh", 1)
    n2 = shifted(both1[:, d:], "zh", -1)
    swaps = []
    for v in (both_own, both3, both1, jnp.concatenate([m2, n2], axis=1)):
        swaps.append(shifted(v, "c", 1))
    arrays = (both_own, swaps[0], both1, swaps[2], both3, swaps[1], swaps[3], m2, n2)

    def spots(k):
        return ((0, k), (1, k), (2, k), (3, k), (7 + k, 0), (6, k), (4, k), (5, k))

    x = lax.axis_index("x").astype(jnp.int32)
    *terms, d_hidden = weight_terms(
        arrays, spots(0), spots(1), act_t, w_out, slope, x.reshape(1), nx, ny, rows, padded
    )
    moved = {}
    for k in (1, 3, 2):
        moved[k] = shifted(terms[k], "x", k)
    dn_own, dn_other = input_grad(d_hidden, w_in, rows, padded)
    from_core = shifted(dn_other, "c", 1)

    def pair(k):
        lanes = slice(k * d, (k + 1) * d)
        return dn_own[:, lanes].astype(F32) + from_core[:, lanes].astype(F32)

    passing = shifted(pair(2).astype(BF), "zh", 1)
    from_up = shifted(pair(3).astype(BF), "zh", -1)
    from_down = shifted((pair(1) + passing.astype(F32)).astype(BF), "zh", 1)
    d_normed = pair(0) + from_up.astype(F32) + from_down.astype(F32)

    p, q = ff // nx, d // ny
    total = terms[0].astype(F32)
    for k in (1, 3, 2):
        total = total + moved[k].astype(F32)
    both_y = lax.all_to_all(total.astype(BF), "y", 0, 0, tiled=True)
    both = jnp.sum(both_y.astype(F32), axis=0).astype(BF)
    got = lax.all_to_all(
        jnp.broadcast_to(both, (nx * nz, *both.shape)), ("x", "zl"), 0, 0, tiled=True
    )
    whole = jnp.sum(got.reshape(nx, nz, 2, p, q).astype(F32), axis=1)

    values = inputs.astype(F32)
    row_mean = jnp.mean(values, axis=1, keepdims=True)
    centred = values - row_mean
    row_var = jnp.mean(centred * centred, axis=1, keepdims=True)
    inv_std = lax.rsqrt(row_var + EPSILON)
    x_hat = centred * inv_std
    d_hat = d_normed * ln_gain
    first_term = jnp.mean(d_hat, axis=1, keepdims=True)
    second_term = jnp.mean(d_hat * x_hat, axis=1, keepdims=True)
    grad_inputs = (
        both_own[:, :d].astype(F32) + inv_std * (d_hat - first_term - x_hat * second_term)
    ).astype(BF)

    scale = float(rows * n * nx * ny * nz) ** (-0.5)
    grad_w_out = whole[:, 1].reshape(ff, q) * scale
    grad_w_in = jnp.transpose(whole[:, 0], (1, 0, 2)).reshape(q, ff) * scale
    return (grad_inputs, grad_w_in, grad_w_out)


RUN = 3


def solution(mesh):
    dp, seq, mp = (mesh.shape[a] for a in ("dp", "seq", "mp"))
    fine = Mesh(mesh.devices.reshape(dp // RUN, RUN, seq, mp // 2, 2), ("x", "zl", "y", "zh", "c"))
    tokens = ("x", "zl", "y")
    hidden = ("zh", "c")

    return jax.shard_map(
        shards,
        mesh=fine,
        in_specs=(
            P((*tokens, *hidden), None),
            P((*tokens, *hidden), None),
            P((*tokens, *hidden)),
            P(tokens, hidden),
            P(None, hidden),
            P(hidden, None),
            P(),
            P(),
        ),
        out_specs=(P((*tokens, *hidden), None), P("y", hidden), P(hidden, "y")),
        check_vma=False,
    )
```

time: 246 us -> 196 us (0.80)
  the two profiles are of different devices: /device:TPU:192 before, /device:TPU:64 now
where the time goes in v1:
time: 196 us; the launch traced here: 195 us
  starting transfers between devices  82.3 us (42%)
  waiting for transfers between devices  80.1 us (41%)
  Pallas kernels  14.1 us (7%)
  other arithmetic  9.38 us (5%)
  local copies, waits for them, and re-layouts  8.33 us (4%)
    ppermute x15, waiting for transfers between devices, shifted(): return lax.ppermute(value, axis, [(i, (i + step) % n) for i in range(n)])  69.6 us
    ppermute x15, starting transfers between devices, shifted(): return lax.ppermute(value, axis, [(i, (i + step) % n) for i in range(n)])  59.3 us
    all_to_all x1, starting transfers between devices, shards(): lax.all_to_all(jnp.broadcast_to(both, (nx * nz, *both.shape)), ('x', 'zl'...  16 us
    pallas_call x2, Pallas kernels, in_hbm(): pl.pallas_call(whole, out_shape=[pltpu.HBM(v.shape, v.dtype) for v in out...  11.9 us
    all_to_all x1, waiting for transfers between devices, shards(): both_y = lax.all_to_all(total.astype(BF), 'y', 0, 0, tiled=True)  10.5 us
    all_to_all x1, starting transfers between devices, shards(): both_y = lax.all_to_all(total.astype(BF), 'y', 0, 0, tiled=True)  7.1 us
  transfers between devices with their start and end apart: 17, of which 6 were waited for; matrix products, arithmetic and copies ran while one was open for 5% of the time, Pallas kernels for 2%

profile of v1, /device:TPU:64, one launch (start us, length us, event | category | flops | bytes accessed | tf_op | source)
XLA Modules:
  0.0 195.2 jit_solution(4637184264451020059)
XLA Ops:
  0.6 1.5 copy.19.m_ref
  2.1 2.1 %shard_map.103.refs_1_ = bf16[98,2048]{1,0:T(8,128)(2,1)} custom-call(bf16[98,1024]{1,0:T(8,128)(2,1)} %x_ref.1, bf16[98,1024]{1,0:T(8,128)(2,1)} %g_ref.1, s32[98,1]{1,0:T(8,128)} %copy.19.m_ref, f32[1,1024]{1,0:T(1,128)} %bitcast.28, f32[1,1024]{1,0:T(1,128)} %bitcast.29), custom_call_target="tpu_custom_call" | custom-call | tf_op jit(solution)/shard_map/pallas_call | solution.py:94
  4.2 9.2 %collective-permute-start.3 = (bf16[98,2048]{1,0:T(8,128)(2,1)}, bf16[98,2048]{1,0:T(8,128)(2,1)S(1)}, u32[]{:S(2)}, u32[]{:S(2)}) collective-permute-start(bf16[98,2048]{1,0:T(8,128)(2,1)} %shard_map.103.refs_1_), channel_id=1, source_target_pairs={{0,2},{2,4},{4,6},{6,0},{1,3},{3,5},{5,7},{7,1},{8,10},{10,12},{12... | collective-permute-start | bytes 1204232 | tf_op jit(solution)/shard_map/ppermute | solution.py:21
  13.4 6.5 %collective-permute-start.1 = (bf16[98,2048]{1,0:T(8,128)(2,1)}, bf16[98,2048]{1,0:T(8,128)(2,1)S(1)}, u32[]{:S(2)}, u32[]{:S(2)}) collective-permute-start(bf16[98,2048]{1,0:T(8,128)(2,1)} %shard_map.103.refs_1_), channel_id=1, source_target_pairs={{0,6},{2,0},{4,2},{6,4},{1,7},{3,1},{5,3},{7,5},{8,14},{10,8},{12,... | collective-permute-start | bytes 1204232 | tf_op jit(solution)/shard_map/ppermute | solution.py:21
  19.9 20.5 %collective-permute-done.3.refs_5_ = bf16[98,2048]{1,0:T(8,128)(2,1)S(1)} collective-permute-done((bf16[98,2048]{1,0:T(8,128)(2,1)}, bf16[98,2048]{1,0:T(8,128)(2,1)S(1)}, u32[]{:S(2)}, u32[]{:S(2)}) %collective-permute-start.3) | collective-permute-done | bytes 401440 | tf_op jit(solution)/shard_map/ppermute | solution.py:21
  40.4 0.8 slice.65
  41.1 1.9 collective-permute-start.5
  43.1 0.7 slice.66
  43.8 6.9 %collective-permute-start.6 = (bf16[98,1024]{1,0:T(8,128)(2,1)}, bf16[98,1024]{1,0:T(8,128)(2,1)}, u32[]{:S(2)}, u32[]{:S(2)}) collective-permute-start(bf16[98,1024]{1,0:T(8,128)(2,1)} %slice.66), channel_id=1, source_target_pairs={{0,6},{2,0},{4,2},{6,4},{1,7},{3,1},{5,3},{7,5},{8,14},{10,8},{12,... | collective-permute-start | bytes 602120 | tf_op jit(solution)/shard_map/ppermute | solution.py:21
  50.8 1.9 collective-permute-start
  52.7 0.2 reshape.51
  52.9 0.1 slice.52
  53.1 0.3 fusion.9
  53.5 0.7 copy-done.5
  54.1 2.4 %collective-permute-start.2 = (bf16[98,2048]{1,0:T(8,128)(2,1)S(1)}, bf16[98,2048]{1,0:T(8,128)(2,1)S(1)}, u32[]{:S(2)}, u32[]{:S(2)}) collective-permute-start(bf16[98,2048]{1,0:T(8,128)(2,1)S(1)} %copy-done.5), channel_id=1, source_target_pairs={{0,1},{1,0},{2,3},{3,2},{4,5},{5,4},{6,7},{7,6},{8,9},{9,8},{10,11... | collective-permute-start | bytes 1204232 | tf_op jit(solution)/shard_map/ppermute | solution.py:21
  56.5 1.9 collective-permute-start.4
  58.5 1.8 pad_maximum_fusion
  60.3 2.4 %collective-permute-start.7 = (bf16[98,2048]{1,0:T(8,128)(2,1)}, bf16[98,2048]{1,0:T(8,128)(2,1)}, u32[]{:S(2)}, u32[]{:S(2)}) collective-permute-start(bf16[98,2048]{1,0:T(8,128)(2,1)} %pad_maximum_fusion), channel_id=1, source_target_pairs={{0,1},{1,0},{2,3},{3,2},{4,5},{5,4},{6,7},{7,6},{8,9},{9,8},{10,11... | collective-permute-start | bytes 1204232 | tf_op jit(solution)/shard_map/ppermute | solution.py:21
  62.7 0.3 fusion.8
  63.1 2.1 %fusion.6 = (f32[896,512]{1,0:T(8,128)}, bf16[512,896]{0,1:T(8,128)(2,1)S(1)}) fusion(bf16[8,112,512]{2,1,0:T(8,128)(2,1)S(1)} %pad.4), kind=kLoop, calls=%fused_computation.11 | loop fusion | flops 5046272 | bytes 3670016 | tf_op jit(solution)/shard_map/add | solution.py:28
  65.2 1.3 copy.20.refs_10_
  66.5 0.7 copy-done.7
  67.2 0.2 copy-done.8
  67.4 8.1 %shard_map.104 = (bf16[8,256,128]{2,1,0:T(8,128)(2,1)}, bf16[8,256,128]{2,1,0:T(8,128)(2,1)}, bf16[8,256,128]{2,1,0:T(8,128)(2,1)}, bf16[8,256,128]{2,1,0:T(8,128)(2,1)}, bf16[896,512]{1,0:T(8,128)(2,1)}) custom-call(s32[1]{0:T(128)} %bitcast.3.refs_0_, bf16[98,2048]{1,0:T(8,128)(2,1)} %shard_map.103.refs_1_, bf16[98,2048]{1,0:T(8,128)(2,1)} %collective-permute-done.refs_2_, ...), custom_call_target="tpu_custom_call" | custom-call | tf_op jit(solution)/shard_map/pallas_call | solution.py:55
  75.5 3.4 %collective-permute-start.12 = (bf16[8,256,128]{2,1,0:T(8,128)(2,1)}, bf16[8,256,128]{2,1,0:T(8,128)(2,1)S(1)}, u32[]{:S(2)}, u32[]{:S(2)}) collective-permute-start(bf16[8,256,128]{2,1,0:T(8,128)(2,1)} %get-tuple-element.14), channel_id=1, source_target_pairs={{0,192},{192,384},{384,576},{576,0},{1,193},{193,385},{385,577},{5... | collective-permute-start | bytes 1572872 | tf_op jit(solution)/shard_map/ppermute | solution.py:21
  78.9 3.7 %collective-permute-start.13 = (bf16[8,256,128]{2,1,0:T(8,128)(2,1)}, bf16[8,256,128]{2,1,0:T(8,128)(2,1)S(1)}, u32[]{:S(2)}, u32[]{:S(2)}) collective-permute-start(bf16[8,256,128]{2,1,0:T(8,128)(2,1)} %get-tuple-element.15), channel_id=1, source_target_pairs={{0,576},{192,0},{384,192},{576,384},{1,577},{193,1},{385,193},{577... | collective-permute-start | bytes 1572872 | tf_op jit(solution)/shard_map/ppermute | solution.py:21
  82.6 3.7 %collective-permute-start.14 = (bf16[8,256,128]{2,1,0:T(8,128)(2,1)}, bf16[8,256,128]{2,1,0:T(8,128)(2,1)S(1)}, u32[]{:S(2)}, u32[]{:S(2)}) collective-permute-start(bf16[8,256,128]{2,1,0:T(8,128)(2,1)} %get-tuple-element.16), channel_id=1, source_target_pairs={{0,384},{192,576},{384,0},{576,192},{1,385},{193,577},{385,1},{577... | collective-permute-start | bytes 1572872 | tf_op jit(solution)/shard_map/ppermute | solution.py:21
  86.3 6.4 %collective-permute-done.12 = bf16[8,256,128]{2,1,0:T(8,128)(2,1)S(1)} collective-permute-done((bf16[8,256,128]{2,1,0:T(8,128)(2,1)}, bf16[8,256,128]{2,1,0:T(8,128)(2,1)S(1)}, u32[]{:S(2)}, u32[]{:S(2)}) %collective-permute-start.12) | collective-permute-done | bytes 524320 | tf_op jit(solution)/shard_map/ppermute | solution.py:21
  92.7 12.6 %collective-permute-done.13 = bf16[8,256,128]{2,1,0:T(8,128)(2,1)S(1)} collective-permute-done((bf16[8,256,128]{2,1,0:T(8,128)(2,1)}, bf16[8,256,128]{2,1,0:T(8,128)(2,1)S(1)}, u32[]{:S(2)}, u32[]{:S(2)}) %collective-permute-start.13) | collective-permute-done | bytes 524320 | tf_op jit(solution)/shard_map/ppermute | solution.py:21
  105.2 2.1 %add_convert_fusion = bf16[8,256,128]{2,1,0:T(8,128)(2,1)} fusion(bf16[8,256,128]{2,1,0:T(8,128)(2,1)S(1)} %collective-permute-done.14, bf16[8,256,128]{2,1,0:T(8,128)(2,1)S(1)} %collective-permute-done.13, bf16[8,256,128]{2,1,0:T(8,128)(2,1)S(1)} %collective-permute-done.12, bf16[8,256,128]{2,1,0:T(8,128)(2,1)} %get-tuple-element.13), kind=kLoop, calls=%fused_computation.17 | loop fusion | flops 2097152 | bytes 2621440 | tf_op jit(solution)/shard_map/convert_element_type | solution.py:210
  107.4 7.1 %all-to-all-start = ((bf16[8,256,128]{2,1,0:T(8,128)(2,1)}), bf16[8,256,128]{2,1,0:T(8,128)(2,1)S(1)}, u32[]{:S(2)}, u32[]{:S(2)}) async-start(bf16[8,256,128]{2,1,0:T(8,128)(2,1)} %add_convert_fusion), calls=%async_computation | async-start | bytes 1048576 | tf_op jit(solution)/shard_map/all_to_all | solution.py:210
  114.5 3.9 %shard_map.105 = (bf16[98,4096]{1,0:T(8,128)(2,1)}, bf16[98,4096]{1,0:T(8,128)(2,1)}) custom-call(bf16[896,512]{1,0:T(8,128)(2,1)} %get-tuple-element.10.refs_0_, bf16[1024,512]{1,0:T(8,128)(2,1)} %refs_1_.1), custom_call_target="tpu_custom_call" | custom-call | tf_op jit(solution)/shard_map/pallas_call | solution.py:55
  118.4 2.1 %collective-permute-start.8 = (bf16[98,4096]{1,0:T(8,128)(2,1)}, bf16[98,4096]{1,0:T(8,128)(2,1)S(1)}, u32[]{:S(2)}, u32[]{:S(2)}) collective-permute-start(bf16[98,4096]{1,0:T(8,128)(2,1)} %get-tuple-element.12), channel_id=1, source_target_pairs={{0,1},{1,0},{2,3},{3,2},{4,5},{5,4},{6,7},{7,6},{8,9},{9,8},{10,11... | collective-permute-start | bytes 2408456 | tf_op jit(solution)/shard_map/ppermute | solution.py:21
  120.4 10.5 %all-to-all-done = bf16[8,256,128]{2,1,0:T(8,128)(2,1)S(1)} async-done(((bf16[8,256,128]{2,1,0:T(8,128)(2,1)}), bf16[8,256,128]{2,1,0:T(8,128)(2,1)S(1)}, u32[]{:S(2)}, u32[]{:S(2)}) %all-to-all-start) | async-done | bytes 524320 | tf_op jit(solution)/shard_map/all_to_all | solution.py:210
  131.0 1.0 broadcast_in_dim.20
  132.1 16.0 %all-to-all-start.1 = ((bf16[12,256,128]{2,1,0:T(8,128)(2,1)}), bf16[12,256,128]{2,1,0:T(8,128)(2,1)S(1)}, u32[]{:S(2)}, u32[]{:S(2)}) async-start(bf16[12,256,128]{2,1,0:T(8,128)(2,1)} %broadcast_in_dim.20), calls=%async_computation.1 | async-start | bytes 1572864 | tf_op jit(solution)/shard_map/all_to_all | solution.py:212
  148.2 0.2 add_convert_fusion.3
  148.3 6.6 %collective-permute-start.10 = (bf16[98,1024]{1,0:T(8,128)(2,1)S(1)}, bf16[98,1024]{1,0:T(8,128)(2,1)S(1)}, u32[]{:S(2)}, u32[]{:S(2)}) collective-permute-start(bf16[98,1024]{1,0:T(8,128)(2,1)S(1)} %get-tuple-element.24), channel_id=1, source_target_pairs={{0,2},{2,4},{4,6},{6,0},{1,3},{3,5},{5,7},{7,1},{8,10},{10,12},{12... | collective-permute-start | bytes 602120 | tf_op jit(solution)/shard_map/ppermute | solution.py:21
  155.0 0.2 fusion.19
  155.2 2.2 %collective-permute-start.9 = (bf16[98,1024]{1,0:T(8,128)(2,1)S(1)}, bf16[98,1024]{1,0:T(8,128)(2,1)S(1)}, u32[]{:S(2)}, u32[]{:S(2)}) collective-permute-start(bf16[98,1024]{1,0:T(8,128)(2,1)S(1)} %get-tuple-element.23), channel_id=1, source_target_pairs={{0,6},{2,0},{4,2},{6,4},{1,7},{3,1},{5,3},{7,5},{8,14},{10,8},{12,... | collective-permute-start | bytes 602120 | tf_op jit(solution)/shard_map/ppermute | solution.py:21
  157.4 23.9 %collective-permute-done.10 = bf16[98,1024]{1,0:T(8,128)(2,1)S(1)} collective-permute-done((bf16[98,1024]{1,0:T(8,128)(2,1)S(1)}, bf16[98,1024]{1,0:T(8,128)(2,1)S(1)}, u32[]{:S(2)}, u32[]{:S(2)}) %collective-permute-start.10) | collective-permute-done | bytes 200736 | tf_op jit(solution)/shard_map/ppermute | solution.py:21
  181.4 4.4 %collective-permute-start.11 = (bf16[98,1024]{1,0:T(8,128)(2,1)S(1)}, bf16[98,1024]{1,0:T(8,128)(2,1)S(1)}, u32[]{:S(2)}, u32[]{:S(2)}) collective-permute-start(bf16[98,1024]{1,0:T(8,128)(2,1)S(1)} %add_convert_fusion.1), channel_id=1, source_target_pairs={{0,2},{2,4},{4,6},{6,0},{1,3},{3,5},{5,7},{7,1},{8,10},{10,12},{12... | collective-permute-start | bytes 602120 | tf_op jit(solution)/shard_map/ppermute | solution.py:21
  185.8 6.3 %collective-permute-done.11 = bf16[98,1024]{1,0:T(8,128)(2,1)S(1)} collective-permute-done((bf16[98,1024]{1,0:T(8,128)(2,1)S(1)}, bf16[98,1024]{1,0:T(8,128)(2,1)S(1)}, u32[]{:S(2)}, u32[]{:S(2)}) %collective-permute-start.11) | collective-permute-done | bytes 200736 | tf_op jit(solution)/shard_map/ppermute | solution.py:21
  192.1 0.3 fusion.21
  192.4 0.9 fusion.18
  193.5 0.8 slice_multiply_fusion
  194.2 0.1 copy.21
  194.3 0.8 copy.22
  (39 shorter events, 0.6 us)
Async XLA Ops:
  0.6 52.1 %copy-start.2 = (bf16[784,512]{1,0:T(8,128)(2,1)S(1)}, bf16[784,512]{1,0:T(8,128)(2,1)}, u32[]{:S(2)}) copy-start(bf16[784,512]{1,0:T(8,128)(2,1)} %param.11) | copy-start | bytes 2408452
  4.2 48.7 %slice-start = ((bf16[784,512]{1,0:T(8,128)(2,1)}), bf16[588,512]{1,0:T(8,128)(2,1)S(1)}, s32[]{:S(2)}) async-start(bf16[784,512]{1,0:T(8,128)(2,1)} %param.11), calls=%async_computation.2 | async-start | bytes 1212416 | tf_op jit(solution)/shard_map/slice | solution.py:171
  4.2 36.2 %collective-permute-start.3 = (bf16[98,2048]{1,0:T(8,128)(2,1)}, bf16[98,2048]{1,0:T(8,128)(2,1)S(1)}, u32[]{:S(2)}, u32[]{:S(2)}) collective-permute-start(bf16[98,2048]{1,0:T(8,128)(2,1)} %shard_map.103.refs_1_), channel_id=1, source_target_pairs={{0,2},{2,4},{4,6},{6,0},{1,3},{3,5},{5,7},{7,1},{8,10},{10,12},{12... | collective-permute-start | bytes 1204232 | tf_op jit(solution)/shard_map/ppermute | solution.py:21
  13.4 29.6 %collective-permute-start.1 = (bf16[98,2048]{1,0:T(8,128)(2,1)}, bf16[98,2048]{1,0:T(8,128)(2,1)S(1)}, u32[]{:S(2)}, u32[]{:S(2)}) collective-permute-start(bf16[98,2048]{1,0:T(8,128)(2,1)} %shard_map.103.refs_1_), channel_id=1, source_target_pairs={{0,6},{2,0},{4,2},{6,4},{1,7},{3,1},{5,3},{7,5},{8,14},{10,8},{12,... | collective-permute-start | bytes 1204232 | tf_op jit(solution)/shard_map/ppermute | solution.py:21
  40.4 16.1 %copy-start.3 = (bf16[98,2048]{1,0:T(8,128)(2,1)}, bf16[98,2048]{1,0:T(8,128)(2,1)S(1)}, u32[]{:S(2)}) copy-start(bf16[98,2048]{1,0:T(8,128)(2,1)S(1)} %collective-permute-done.3.refs_5_) | copy-start | bytes 1204228
  41.1 17.3 %collective-permute-start.5 = (bf16[98,1024]{1,0:T(8,128)(2,1)}, bf16[98,1024]{1,0:T(8,128)(2,1)}, u32[]{:S(2)}, u32[]{:S(2)}) collective-permute-start(bf16[98,1024]{1,0:T(8,128)(2,1)} %slice.65), channel_id=1, source_target_pairs={{0,2},{2,4},{4,6},{6,0},{1,3},{3,5},{5,7},{7,1},{8,10},{10,12},{12... | collective-permute-start | bytes 602120 | tf_op jit(solution)/shard_map/ppermute | solution.py:21
  43.1 9.6 %copy-start.4 = (bf16[98,2048]{1,0:T(8,128)(2,1)}, bf16[98,2048]{1,0:T(8,128)(2,1)S(1)}, u32[]{:S(2)}) copy-start(bf16[98,2048]{1,0:T(8,128)(2,1)S(1)} %collective-permute-done.1.refs_3_) | copy-start | bytes 1204228
  43.8 14.6 %collective-permute-start.6 = (bf16[98,1024]{1,0:T(8,128)(2,1)}, bf16[98,1024]{1,0:T(8,128)(2,1)}, u32[]{:S(2)}, u32[]{:S(2)}) collective-permute-start(bf16[98,1024]{1,0:T(8,128)(2,1)} %slice.66), channel_id=1, source_target_pairs={{0,6},{2,0},{4,2},{6,4},{1,7},{3,1},{5,3},{7,5},{8,14},{10,8},{12,... | collective-permute-start | bytes 602120 | tf_op jit(solution)/shard_map/ppermute | solution.py:21
  50.8 15.7 %collective-permute-start = (bf16[98,2048]{1,0:T(8,128)(2,1)}, bf16[98,2048]{1,0:T(8,128)(2,1)}, u32[]{:S(2)}, u32[]{:S(2)}) collective-permute-start(bf16[98,2048]{1,0:T(8,128)(2,1)} %shard_map.103.refs_1_), channel_id=1, source_target_pairs={{0,1},{1,0},{2,3},{3,2},{4,5},{5,4},{6,7},{7,6},{8,9},{9,8},{10,11... | collective-permute-start | bytes 1204232 | tf_op jit(solution)/shard_map/ppermute | solution.py:21
  53.1 1.0 copy-start.5
  54.1 12.4 %collective-permute-start.2 = (bf16[98,2048]{1,0:T(8,128)(2,1)S(1)}, bf16[98,2048]{1,0:T(8,128)(2,1)S(1)}, u32[]{:S(2)}, u32[]{:S(2)}) collective-permute-start(bf16[98,2048]{1,0:T(8,128)(2,1)S(1)} %copy-done.5), channel_id=1, source_target_pairs={{0,1},{1,0},{2,3},{3,2},{4,5},{5,4},{6,7},{7,6},{8,9},{9,8},{10,11... | collective-permute-start | bytes 1204232 | tf_op jit(solution)/shard_map/ppermute | solution.py:21
  56.5 9.9 %collective-permute-start.4 = (bf16[98,2048]{1,0:T(8,128)(2,1)S(1)}, bf16[98,2048]{1,0:T(8,128)(2,1)S(1)}, u32[]{:S(2)}, u32[]{:S(2)}) collective-permute-start(bf16[98,2048]{1,0:T(8,128)(2,1)S(1)} %collective-permute-done.3.refs_5_), channel_id=1, source_target_pairs={{0,1},{1,0},{2,3},{3,2},{4,5},{5,4},{6,7},{7,6},{8,9},{9,8},{10,11... | collective-permute-start | bytes 1204232 | tf_op jit(solution)/shard_map/ppermute | solution.py:21
  60.3 6.2 %collective-permute-start.7 = (bf16[98,2048]{1,0:T(8,128)(2,1)}, bf16[98,2048]{1,0:T(8,128)(2,1)}, u32[]{:S(2)}, u32[]{:S(2)}) collective-permute-start(bf16[98,2048]{1,0:T(8,128)(2,1)} %pad_maximum_fusion), channel_id=1, source_target_pairs={{0,1},{1,0},{2,3},{3,2},{4,5},{5,4},{6,7},{7,6},{8,9},{9,8},{10,11... | collective-permute-start | bytes 1204232 | tf_op jit(solution)/shard_map/ppermute | solution.py:21
  66.5 0.8 copy-start.7
  66.5 1.0 copy-start.8
  75.5 17.2 %collective-permute-start.12 = (bf16[8,256,128]{2,1,0:T(8,128)(2,1)}, bf16[8,256,128]{2,1,0:T(8,128)(2,1)S(1)}, u32[]{:S(2)}, u32[]{:S(2)}) collective-permute-start(bf16[8,256,128]{2,1,0:T(8,128)(2,1)} %get-tuple-element.14), channel_id=1, source_target_pairs={{0,192},{192,384},{384,576},{576,0},{1,193},{193,385},{385,577},{5... | collective-permute-start | bytes 1572872 | tf_op jit(solution)/shard_map/ppermute | solution.py:21
  78.9 26.3 %collective-permute-start.13 = (bf16[8,256,128]{2,1,0:T(8,128)(2,1)}, bf16[8,256,128]{2,1,0:T(8,128)(2,1)S(1)}, u32[]{:S(2)}, u32[]{:S(2)}) collective-permute-start(bf16[8,256,128]{2,1,0:T(8,128)(2,1)} %get-tuple-element.15), channel_id=1, source_target_pairs={{0,576},{192,0},{384,192},{576,384},{1,577},{193,1},{385,193},{577... | collective-permute-start | bytes 1572872 | tf_op jit(solution)/shard_map/ppermute | solution.py:21
  82.6 22.6 %collective-permute-start.14 = (bf16[8,256,128]{2,1,0:T(8,128)(2,1)}, bf16[8,256,128]{2,1,0:T(8,128)(2,1)S(1)}, u32[]{:S(2)}, u32[]{:S(2)}) collective-permute-start(bf16[8,256,128]{2,1,0:T(8,128)(2,1)} %get-tuple-element.16), channel_id=1, source_target_pairs={{0,384},{192,576},{384,0},{576,192},{1,385},{193,577},{385,1},{577... | collective-permute-start | bytes 1572872 | tf_op jit(solution)/shard_map/ppermute | solution.py:21
  107.4 23.6 %all-to-all-start = ((bf16[8,256,128]{2,1,0:T(8,128)(2,1)}), bf16[8,256,128]{2,1,0:T(8,128)(2,1)S(1)}, u32[]{:S(2)}, u32[]{:S(2)}) async-start(bf16[8,256,128]{2,1,0:T(8,128)(2,1)} %add_convert_fusion), calls=%async_computation | async-start | bytes 1048576 | tf_op jit(solution)/shard_map/all_to_all | solution.py:210
  118.3 29.7 %copy-start = (bf16[98,1024]{1,0:T(8,128)(2,1)S(1)}, bf16[98,1024]{1,0:T(8,128)(2,1)}, u32[]{:S(2)}) copy-start(bf16[98,1024]{1,0:T(8,128)(2,1)} %x_ref.1) | copy-start | bytes 602116
  118.4 29.8 %copy-start.6 = (bf16[98,4096]{1,0:T(8,128)(2,1)S(1)}, bf16[98,4096]{1,0:T(8,128)(2,1)}, u32[]{:S(2)}) copy-start(bf16[98,4096]{1,0:T(8,128)(2,1)} %get-tuple-element.11) | copy-start | bytes 2408452
  118.4 29.8 %collective-permute-start.8 = (bf16[98,4096]{1,0:T(8,128)(2,1)}, bf16[98,4096]{1,0:T(8,128)(2,1)S(1)}, u32[]{:S(2)}, u32[]{:S(2)}) collective-permute-start(bf16[98,4096]{1,0:T(8,128)(2,1)} %get-tuple-element.12), channel_id=1, source_target_pairs={{0,1},{1,0},{2,3},{3,2},{4,5},{5,4},{6,7},{7,6},{8,9},{9,8},{10,11... | collective-permute-start | bytes 2408456 | tf_op jit(solution)/shard_map/ppermute | solution.py:21
  132.1 60.1 %copy-start.9 = (f32[1024]{0:T(1024)S(1)}, f32[1024]{0:T(1024)}, u32[]{:S(2)}) copy-start(f32[1024]{0:T(1024)} %param.14) | copy-start | bytes 12292
  132.1 61.3 %all-to-all-start.1 = ((bf16[12,256,128]{2,1,0:T(8,128)(2,1)}), bf16[12,256,128]{2,1,0:T(8,128)(2,1)S(1)}, u32[]{:S(2)}, u32[]{:S(2)}) async-start(bf16[12,256,128]{2,1,0:T(8,128)(2,1)} %broadcast_in_dim.20), calls=%async_computation.1 | async-start | bytes 1572864 | tf_op jit(solution)/shard_map/all_to_all | solution.py:212
  148.2 44.3 %copy-start.1 = (bf16[98,2048]{1,0:T(8,128)(2,1)S(1)}, bf16[98,2048]{1,0:T(8,128)(2,1)}, u32[]{:S(2)}) copy-start(bf16[98,2048]{1,0:T(8,128)(2,1)} %shard_map.103.refs_1_) | copy-start | bytes 1204228
  148.3 32.9 %collective-permute-start.10 = (bf16[98,1024]{1,0:T(8,128)(2,1)S(1)}, bf16[98,1024]{1,0:T(8,128)(2,1)S(1)}, u32[]{:S(2)}, u32[]{:S(2)}) collective-permute-start(bf16[98,1024]{1,0:T(8,128)(2,1)S(1)} %get-tuple-element.24), channel_id=1, source_target_pairs={{0,2},{2,4},{4,6},{6,0},{1,3},{3,5},{5,7},{7,1},{8,10},{10,12},{12... | collective-permute-start | bytes 602120 | tf_op jit(solution)/shard_map/ppermute | solution.py:21
  155.2 30.6 %collective-permute-start.9 = (bf16[98,1024]{1,0:T(8,128)(2,1)S(1)}, bf16[98,1024]{1,0:T(8,128)(2,1)S(1)}, u32[]{:S(2)}, u32[]{:S(2)}) collective-permute-start(bf16[98,1024]{1,0:T(8,128)(2,1)S(1)} %get-tuple-element.23), channel_id=1, source_target_pairs={{0,6},{2,0},{4,2},{6,4},{1,7},{3,1},{5,3},{7,5},{8,14},{10,8},{12,... | collective-permute-start | bytes 602120 | tf_op jit(solution)/shard_map/ppermute | solution.py:21
  181.4 10.7 %collective-permute-start.11 = (bf16[98,1024]{1,0:T(8,128)(2,1)S(1)}, bf16[98,1024]{1,0:T(8,128)(2,1)S(1)}, u32[]{:S(2)}, u32[]{:S(2)}) collective-permute-start(bf16[98,1024]{1,0:T(8,128)(2,1)S(1)} %add_convert_fusion.1), channel_id=1, source_target_pairs={{0,2},{2,4},{4,6},{6,0},{1,3},{3,5},{5,7},{7,1},{8,10},{10,12},{12... | collective-permute-start | bytes 602120 | tf_op jit(solution)/shard_map/ppermute | solution.py:21

commit v2 on v1

--- a/solution.py
+++ b/solution.py
@@ -36,7 +36,7 @@
     return lax.dot_general(a, b, dims, preferred_element_type=F32)
 
 
-def in_hbm(body, outs, scratch, fetched, smem=()):
+def in_hbm(body, outs, scratch, fetched, smem=(), loose=()):
     ni, no, ns = len(fetched), len(outs), len(smem)
 
     def whole(*refs):
@@ -55,7 +55,8 @@
     return pl.pallas_call(
         whole,
         out_shape=[pltpu.HBM(v.shape, v.dtype) for v in outs],
-        in_specs=[pl.BlockSpec(memory_space=pltpu.SMEM)] * ns + [hbm] * ni,
+        in_specs=[pl.BlockSpec(memory_space=pltpu.SMEM)] * ns
+        + [pl.BlockSpec(memory_space=pl.ANY) if k in loose else hbm for k in range(ni)],
         out_specs=[hbm] * no,
         scratch_shapes=[
             pltpu.SemaphoreType.DMA((ni,)),
@@ -64,7 +65,13 @@
             *scratch,
         ],
         compiler_params=pltpu.CompilerParams(vmem_limit_bytes=LIMIT),
-    )(*smem, *(pltpu.with_memory_space_constraint(v, pltpu.HBM) for v in fetched))
+    )(
+        *smem,
+        *(
+            v if k in loose else pltpu.with_memory_space_constraint(v, pltpu.HBM)
+            for k, v in enumerate(fetched)
+        ),
+    )
 
 
 def shaped(shape, dtype=BF):
@@ -87,7 +94,10 @@
         centred = values - jnp.mean(values, axis=1, keepdims=True)
         row_var = jnp.mean(centred * centred, axis=1, keepdims=True)
         x_hat = centred * lax.rsqrt(row_var + EPSILON)
-        out_ref[:, :d] = (g_ref[...].astype(F32) * m_ref[...].astype(F32)).astype(BF)
+        square = [lax.broadcasted_iota(jnp.int32, (rows, rows), k) for k in (0, 1)]
+        diagonal = jnp.where(square[0] == square[1], m_ref[...].astype(F32), 0.0)
+        mask = jnp.sum(diagonal, axis=1, keepdims=True)
+        out_ref[:, :d] = (g_ref[...].astype(F32) * mask).astype(BF)
         out_ref[:, d:] = (x_hat * gain_ref[...] + shift_ref[...]).astype(BF)
 
     vmem = pl.BlockSpec(memory_space=pltpu.VMEM)
@@ -96,7 +106,7 @@
         out_shape=shaped((rows, 2 * d)),
         in_specs=[vmem] * 5,
         out_specs=vmem,
-    )(inputs, grad_out, pad_mask[:, None], ln_gain[None], ln_shift[None])
+    )(inputs, grad_out, pad_mask[None], ln_gain[None], ln_shift[None])
 
 
 def weight_terms(arrays, m_spots, n_spots, act_t, w_out, slope, x_idx, nx, ny, rows, padded):
@@ -134,6 +144,7 @@
         [pltpu.VMEM((total, d), BF), pltpu.VMEM((total, d), BF), pltpu.VMEM((nx, ny, 2 * q, p), BF)],
         (*arrays, act_t, w_out, slope),
         (x_idx,),
+        (6,),
     )
 
 
@@ -203,7 +214,6 @@
     from_down = shifted((pair(1) + passing.astype(F32)).astype(BF), "zh", 1)
     d_normed = pair(0) + from_up.astype(F32) + from_down.astype(F32)
 
-    p, q = ff // nx, d // ny
     total = terms[0].astype(F32)
     for k in (1, 3, 2):
         total = total + moved[k].astype(F32)
@@ -212,7 +222,11 @@
     got = lax.all_to_all(
         jnp.broadcast_to(both, (nx * nz, *both.shape)), ("x", "zl"), 0, 0, tiled=True
     )
-    whole = jnp.sum(got.reshape(nx, nz, 2, p, q).astype(F32), axis=1)
+    p, q = ff // nx, d // ny
+    scale = float(rows * n * nx * ny * nz) ** (-0.5)
+    whole = jnp.sum(got.reshape(nx, nz, 2, q, p).astype(F32), axis=1)
+    grad_w_in = jnp.transpose(whole[:, 0], (1, 0, 2)).reshape(q, ff) * scale
+    grad_w_out = whole[:, 1].reshape(ff, q) * scale
 
     values = inputs.astype(F32)
     row_mean = jnp.mean(values, axis=1, keepdims=True)
@@ -227,9 +241,6 @@
         both_own[:, :d].astype(F32) + inv_std * (d_hat - first_term - x_hat * second_term)
     ).astype(BF)
 
-    scale = float(rows * n * nx * ny * nz) ** (-0.5)
-    grad_w_out = whole[:, 1].reshape(ff, q) * scale
-    grad_w_in = jnp.transpose(whole[:, 0], (1, 0, 2)).reshape(q, ff) * scale
     return (grad_inputs, grad_w_in, grad_w_out)
 
 

time: 196 us -> 195 us (level)
  transfers between devices with their start and end apart: 17 -> 17, of which waited for: 6 -> 6; matrix products, arithmetic and copies ran while one was open for 5% -> 6% of each run, Pallas kernels for 2% -> 2%
where the time goes in v2:
time: 195 us; the launch traced here: 194 us
  starting transfers between devices  82.5 us (42%)
  waiting for transfers between devices  80.4 us (41%)
  Pallas kernels  14 us (7%)
  other arithmetic  9.35 us (5%)
  local copies, waits for them, and re-layouts  7.06 us (4%)
    ppermute x15, waiting for transfers between devices, shifted(): return lax.ppermute(value, axis, [(i, (i + step) % n) for i in range(n)])  69.9 us
    ppermute x15, starting transfers between devices, shifted(): return lax.ppermute(value, axis, [(i, (i + step) % n) for i in range(n)])  59.1 us
    all_to_all x1, starting transfers between devices, shards(): lax.all_to_all(jnp.broadcast_to(both, (nx * nz, *both.shape)), ('x', 'zl'...  16.3 us
    pallas_call x2, Pallas kernels, in_hbm(): pl.pallas_call(whole, out_shape=[pltpu.HBM(v.shape, v.dtype) for v in out...  11.9 us
    all_to_all x1, waiting for transfers between devices, shards(): both_y = lax.all_to_all(total.astype(BF), 'y', 0, 0, tiled=True)  10.5 us
    all_to_all x1, starting transfers between devices, shards(): both_y = lax.all_to_all(total.astype(BF), 'y', 0, 0, tiled=True)  7.1 us
  transfers between devices with their start and end apart: 17, of which 6 were waited for; matrix products, arithmetic and copies ran while one was open for 6% of the time, Pallas kernels for 2%

profile of v2, /device:TPU:64, one launch (start us, length us, event | category | flops | bytes accessed | tf_op | source)
XLA Modules:
  0.0 194.4 jit_solution(4779376741716138044)
XLA Ops:
  0.6 2.2 %shard_map.103.refs_1_ = bf16[98,2048]{1,0:T(8,128)(2,1)} custom-call(bf16[98,1024]{1,0:T(8,128)(2,1)} %x_ref.1, bf16[98,1024]{1,0:T(8,128)(2,1)} %g_ref.1, s32[1,98]{1,0:T(1,128)} %bitcast.30, f32[1,1024]{1,0:T(1,128)} %bitcast.28, f32[1,1024]{1,0:T(1,128)} %bitcast.29), custom_call_target="tpu_custom_call" | custom-call | tf_op jit(solution)/shard_map/pallas_call | solution.py:104
  2.8 9.2 %collective-permute-start.3 = (bf16[98,2048]{1,0:T(8,128)(2,1)}, bf16[98,2048]{1,0:T(8,128)(2,1)S(1)}, u32[]{:S(2)}, u32[]{:S(2)}) collective-permute-start(bf16[98,2048]{1,0:T(8,128)(2,1)} %shard_map.103.refs_1_), channel_id=1, source_target_pairs={{0,2},{2,4},{4,6},{6,0},{1,3},{3,5},{5,7},{7,1},{8,10},{10,12},{12... | collective-permute-start | bytes 1204232 | tf_op jit(solution)/shard_map/ppermute | solution.py:21
  12.1 6.5 %collective-permute-start.1 = (bf16[98,2048]{1,0:T(8,128)(2,1)}, bf16[98,2048]{1,0:T(8,128)(2,1)}, u32[]{:S(2)}, u32[]{:S(2)}) collective-permute-start(bf16[98,2048]{1,0:T(8,128)(2,1)} %shard_map.103.refs_1_), channel_id=1, source_target_pairs={{0,6},{2,0},{4,2},{6,4},{1,7},{3,1},{5,3},{7,5},{8,14},{10,8},{12,... | collective-permute-start | bytes 1204232 | tf_op jit(solution)/shard_map/ppermute | solution.py:21
  18.5 20.5 %collective-permute-done.3.refs_5_ = bf16[98,2048]{1,0:T(8,128)(2,1)S(1)} collective-permute-done((bf16[98,2048]{1,0:T(8,128)(2,1)}, bf16[98,2048]{1,0:T(8,128)(2,1)S(1)}, u32[]{:S(2)}, u32[]{:S(2)}) %collective-permute-start.3) | collective-permute-done | bytes 401440 | tf_op jit(solution)/shard_map/ppermute | solution.py:21
  39.0 0.8 slice.65
  39.8 1.9 collective-permute-start.5
  41.7 1.6 slice.66
  43.3 6.9 %collective-permute-start.6 = (bf16[98,1024]{1,0:T(8,128)(2,1)}, bf16[98,1024]{1,0:T(8,128)(2,1)}, u32[]{:S(2)}, u32[]{:S(2)}) collective-permute-start(bf16[98,1024]{1,0:T(8,128)(2,1)} %slice.66), channel_id=1, source_target_pairs={{0,6},{2,0},{4,2},{6,4},{1,7},{3,1},{5,3},{7,5},{8,14},{10,8},{12,... | collective-permute-start | bytes 602120 | tf_op jit(solution)/shard_map/ppermute | solution.py:21
  50.2 1.9 collective-permute-start
  52.2 0.2 reshape.51
  52.4 0.1 slice.52
  52.6 0.3 fusion.9
  52.9 2.4 %collective-permute-start.2 = (bf16[98,2048]{1,0:T(8,128)(2,1)}, bf16[98,2048]{1,0:T(8,128)(2,1)S(1)}, u32[]{:S(2)}, u32[]{:S(2)}) collective-permute-start(bf16[98,2048]{1,0:T(8,128)(2,1)} %collective-permute-done.1.refs_3_), channel_id=1, source_target_pairs={{0,1},{1,0},{2,3},{3,2},{4,5},{5,4},{6,7},{7,6},{8,9},{9,8},{10,11... | collective-permute-start | bytes 1204232 | tf_op jit(solution)/shard_map/ppermute | solution.py:21
  55.4 1.9 collective-permute-start.4
  57.3 1.8 pad_maximum_fusion
  59.1 2.4 %collective-permute-start.7 = (bf16[98,2048]{1,0:T(8,128)(2,1)}, bf16[98,2048]{1,0:T(8,128)(2,1)S(1)}, u32[]{:S(2)}, u32[]{:S(2)}) collective-permute-start(bf16[98,2048]{1,0:T(8,128)(2,1)} %pad_maximum_fusion), channel_id=1, source_target_pairs={{0,1},{1,0},{2,3},{3,2},{4,5},{5,4},{6,7},{7,6},{8,9},{9,8},{10,11... | collective-permute-start | bytes 1204232 | tf_op jit(solution)/shard_map/ppermute | solution.py:21
  61.5 0.3 fusion.8
  61.9 2.1 %fusion.6 = (f32[896,512]{1,0:T(8,128)}, bf16[512,896]{0,1:T(8,128)(2,1)S(1)}) fusion(bf16[8,112,512]{2,1,0:T(8,128)(2,1)S(1)} %pad.4), kind=kLoop, calls=%fused_computation.11 | loop fusion | flops 5046272 | bytes 3670016 | tf_op jit(solution)/shard_map/add | solution.py:28
  64.0 1.3 copy.16.refs_10_
  65.3 0.7 copy-done.6
  66.0 0.2 copy-done.7
  66.2 8.0 %shard_map.104 = (bf16[8,256,128]{2,1,0:T(8,128)(2,1)}, bf16[8,256,128]{2,1,0:T(8,128)(2,1)}, bf16[8,256,128]{2,1,0:T(8,128)(2,1)}, bf16[8,256,128]{2,1,0:T(8,128)(2,1)}, bf16[896,512]{1,0:T(8,128)(2,1)}) custom-call(s32[1]{0:T(128)} %bitcast.3.refs_0_, bf16[98,2048]{1,0:T(8,128)(2,1)} %shard_map.103.refs_1_, bf16[98,2048]{1,0:T(8,128)(2,1)} %collective-permute-done.refs_2_, ...), custom_call_target="tpu_custom_call" | custom-call | tf_op jit(solution)/shard_map/pallas_call | solution.py:55
  74.3 3.4 %collective-permute-start.12 = (bf16[8,256,128]{2,1,0:T(8,128)(2,1)}, bf16[8,256,128]{2,1,0:T(8,128)(2,1)S(1)}, u32[]{:S(2)}, u32[]{:S(2)}) collective-permute-start(bf16[8,256,128]{2,1,0:T(8,128)(2,1)} %get-tuple-element.14), channel_id=1, source_target_pairs={{0,192},{192,384},{384,576},{576,0},{1,193},{193,385},{385,577},{5... | collective-permute-start | bytes 1572872 | tf_op jit(solution)/shard_map/ppermute | solution.py:21
  77.7 3.7 %collective-permute-start.13 = (bf16[8,256,128]{2,1,0:T(8,128)(2,1)}, bf16[8,256,128]{2,1,0:T(8,128)(2,1)S(1)}, u32[]{:S(2)}, u32[]{:S(2)}) collective-permute-start(bf16[8,256,128]{2,1,0:T(8,128)(2,1)} %get-tuple-element.15), channel_id=1, source_target_pairs={{0,576},{192,0},{384,192},{576,384},{1,577},{193,1},{385,193},{577... | collective-permute-start | bytes 1572872 | tf_op jit(solution)/shard_map/ppermute | solution.py:21
  81.3 3.7 %collective-permute-start.14 = (bf16[8,256,128]{2,1,0:T(8,128)(2,1)}, bf16[8,256,128]{2,1,0:T(8,128)(2,1)S(1)}, u32[]{:S(2)}, u32[]{:S(2)}) collective-permute-start(bf16[8,256,128]{2,1,0:T(8,128)(2,1)} %get-tuple-element.16), channel_id=1, source_target_pairs={{0,384},{192,576},{384,0},{576,192},{1,385},{193,577},{385,1},{577... | collective-permute-start | bytes 1572872 | tf_op jit(solution)/shard_map/ppermute | solution.py:21
  85.1 6.4 %collective-permute-done.12 = bf16[8,256,128]{2,1,0:T(8,128)(2,1)S(1)} collective-permute-done((bf16[8,256,128]{2,1,0:T(8,128)(2,1)}, bf16[8,256,128]{2,1,0:T(8,128)(2,1)S(1)}, u32[]{:S(2)}, u32[]{:S(2)}) %collective-permute-start.12) | collective-permute-done | bytes 524320 | tf_op jit(solution)/shard_map/ppermute | solution.py:21
  91.4 12.6 %collective-permute-done.13 = bf16[8,256,128]{2,1,0:T(8,128)(2,1)S(1)} collective-permute-done((bf16[8,256,128]{2,1,0:T(8,128)(2,1)}, bf16[8,256,128]{2,1,0:T(8,128)(2,1)S(1)}, u32[]{:S(2)}, u32[]{:S(2)}) %collective-permute-start.13) | collective-permute-done | bytes 524320 | tf_op jit(solution)/shard_map/ppermute | solution.py:21
  104.0 2.1 %add_convert_fusion = bf16[8,256,128]{2,1,0:T(8,128)(2,1)} fusion(bf16[8,256,128]{2,1,0:T(8,128)(2,1)S(1)} %collective-permute-done.14, bf16[8,256,128]{2,1,0:T(8,128)(2,1)S(1)} %collective-permute-done.13, bf16[8,256,128]{2,1,0:T(8,128)(2,1)S(1)} %collective-permute-done.12, bf16[8,256,128]{2,1,0:T(8,128)(2,1)} %get-tuple-element.13), kind=kLoop, calls=%fused_computation.17 | loop fusion | flops 2097152 | bytes 2621440 | tf_op jit(solution)/shard_map/convert_element_type | solution.py:220
  106.1 7.1 %all-to-all-start = ((bf16[8,256,128]{2,1,0:T(8,128)(2,1)}), bf16[8,256,128]{2,1,0:T(8,128)(2,1)S(1)}, u32[]{:S(2)}, u32[]{:S(2)}) async-start(bf16[8,256,128]{2,1,0:T(8,128)(2,1)} %add_convert_fusion), calls=%async_computation | async-start | bytes 1048576 | tf_op jit(solution)/shard_map/all_to_all | solution.py:220
  113.2 3.9 %shard_map.105 = (bf16[98,4096]{1,0:T(8,128)(2,1)}, bf16[98,4096]{1,0:T(8,128)(2,1)}) custom-call(bf16[896,512]{1,0:T(8,128)(2,1)} %get-tuple-element.10.refs_0_, bf16[1024,512]{1,0:T(8,128)(2,1)} %refs_1_.1), custom_call_target="tpu_custom_call" | custom-call | tf_op jit(solution)/shard_map/pallas_call | solution.py:55
  117.1 2.1 %collective-permute-start.8 = (bf16[98,4096]{1,0:T(8,128)(2,1)}, bf16[98,4096]{1,0:T(8,128)(2,1)S(1)}, u32[]{:S(2)}, u32[]{:S(2)}) collective-permute-start(bf16[98,4096]{1,0:T(8,128)(2,1)} %get-tuple-element.12), channel_id=1, source_target_pairs={{0,1},{1,0},{2,3},{3,2},{4,5},{5,4},{6,7},{7,6},{8,9},{9,8},{10,11... | collective-permute-start | bytes 2408456 | tf_op jit(solution)/shard_map/ppermute | solution.py:21
  119.1 10.5 %all-to-all-done = bf16[8,256,128]{2,1,0:T(8,128)(2,1)S(1)} async-done(((bf16[8,256,128]{2,1,0:T(8,128)(2,1)}), bf16[8,256,128]{2,1,0:T(8,128)(2,1)S(1)}, u32[]{:S(2)}, u32[]{:S(2)}) %all-to-all-start) | async-done | bytes 524320 | tf_op jit(solution)/shard_map/all_to_all | solution.py:220
  129.7 1.0 broadcast_in_dim.20
  130.8 16.3 %all-to-all-start.1 = ((bf16[12,256,128]{2,1,0:T(8,128)(2,1)}), bf16[12,256,128]{2,1,0:T(8,128)(2,1)S(1)}, u32[]{:S(2)}, u32[]{:S(2)}) async-start(bf16[12,256,128]{2,1,0:T(8,128)(2,1)} %broadcast_in_dim.20), calls=%async_computation.1 | async-start | bytes 1572864 | tf_op jit(solution)/shard_map/all_to_all | solution.py:222
  147.1 0.1 convert_reduce_fusion.1
  147.2 0.2 add_convert_fusion.3
  147.4 7.0 %collective-permute-start.10 = (bf16[98,1024]{1,0:T(8,128)(2,1)S(1)}, bf16[98,1024]{1,0:T(8,128)(2,1)S(1)}, u32[]{:S(2)}, u32[]{:S(2)}) collective-permute-start(bf16[98,1024]{1,0:T(8,128)(2,1)S(1)} %get-tuple-element.24), channel_id=1, source_target_pairs={{0,2},{2,4},{4,6},{6,0},{1,3},{3,5},{5,7},{7,1},{8,10},{10,12},{12... | collective-permute-start | bytes 602120 | tf_op jit(solution)/shard_map/ppermute | solution.py:21
  154.4 0.2 fusion.19
  154.6 1.9 collective-permute-start.9
  156.5 24.0 %collective-permute-done.10 = bf16[98,1024]{1,0:T(8,128)(2,1)S(1)} collective-permute-done((bf16[98,1024]{1,0:T(8,128)(2,1)S(1)}, bf16[98,1024]{1,0:T(8,128)(2,1)S(1)}, u32[]{:S(2)}, u32[]{:S(2)}) %collective-permute-start.10) | collective-permute-done | bytes 200736 | tf_op jit(solution)/shard_map/ppermute | solution.py:21
  180.6 4.2 %collective-permute-start.11 = (bf16[98,1024]{1,0:T(8,128)(2,1)S(1)}, bf16[98,1024]{1,0:T(8,128)(2,1)S(1)}, u32[]{:S(2)}, u32[]{:S(2)}) collective-permute-start(bf16[98,1024]{1,0:T(8,128)(2,1)S(1)} %add_convert_fusion.1), channel_id=1, source_target_pairs={{0,2},{2,4},{4,6},{6,0},{1,3},{3,5},{5,7},{7,1},{8,10},{10,12},{12... | collective-permute-start | bytes 602120 | tf_op jit(solution)/shard_map/ppermute | solution.py:21
  184.9 6.5 %collective-permute-done.11 = bf16[98,1024]{1,0:T(8,128)(2,1)S(1)} collective-permute-done((bf16[98,1024]{1,0:T(8,128)(2,1)S(1)}, bf16[98,1024]{1,0:T(8,128)(2,1)S(1)}, u32[]{:S(2)}, u32[]{:S(2)}) %collective-permute-start.11) | collective-permute-done | bytes 200736 | tf_op jit(solution)/shard_map/ppermute | solution.py:21
  191.4 0.3 fusion.21
  191.7 0.9 fusion.18
  192.6 0.1 convert_reduce_fusion
  192.7 0.8 slice_multiply_fusion
  193.5 0.1 copy.17
  193.6 0.8 copy.18
  (36 shorter events, 0.3 us)
Async XLA Ops:
  0.6 51.5 %copy-start.2 = (bf16[784,512]{1,0:T(8,128)(2,1)S(1)}, bf16[784,512]{1,0:T(8,128)(2,1)}, u32[]{:S(2)}) copy-start(bf16[784,512]{1,0:T(8,128)(2,1)} %param.11) | copy-start | bytes 2408452
  2.8 49.6 %slice-start = ((bf16[784,512]{1,0:T(8,128)(2,1)}), bf16[588,512]{1,0:T(8,128)(2,1)S(1)}, s32[]{:S(2)}) async-start(bf16[784,512]{1,0:T(8,128)(2,1)} %param.11), calls=%async_computation.2 | async-start | bytes 1212416 | tf_op jit(solution)/shard_map/slice | solution.py:182
  2.8 36.2 %collective-permute-start.3 = (bf16[98,2048]{1,0:T(8,128)(2,1)}, bf16[98,2048]{1,0:T(8,128)(2,1)S(1)}, u32[]{:S(2)}, u32[]{:S(2)}) collective-permute-start(bf16[98,2048]{1,0:T(8,128)(2,1)} %shard_map.103.refs_1_), channel_id=1, source_target_pairs={{0,2},{2,4},{4,6},{6,0},{1,3},{3,5},{5,7},{7,1},{8,10},{10,12},{12... | collective-permute-start | bytes 1204232 | tf_op jit(solution)/shard_map/ppermute | solution.py:21
  12.1 29.6 %collective-permute-start.1 = (bf16[98,2048]{1,0:T(8,128)(2,1)}, bf16[98,2048]{1,0:T(8,128)(2,1)}, u32[]{:S(2)}, u32[]{:S(2)}) collective-permute-start(bf16[98,2048]{1,0:T(8,128)(2,1)} %shard_map.103.refs_1_), channel_id=1, source_target_pairs={{0,6},{2,0},{4,2},{6,4},{1,7},{3,1},{5,3},{7,5},{8,14},{10,8},{12,... | collective-permute-start | bytes 1204232 | tf_op jit(solution)/shard_map/ppermute | solution.py:21
  39.0 13.4 %copy-start.3 = (bf16[98,2048]{1,0:T(8,128)(2,1)}, bf16[98,2048]{1,0:T(8,128)(2,1)S(1)}, u32[]{:S(2)}) copy-start(bf16[98,2048]{1,0:T(8,128)(2,1)S(1)} %collective-permute-done.3.refs_5_) | copy-start | bytes 1204228
  39.8 17.5 %collective-permute-start.5 = (bf16[98,1024]{1,0:T(8,128)(2,1)}, bf16[98,1024]{1,0:T(8,128)(2,1)}, u32[]{:S(2)}, u32[]{:S(2)}) collective-permute-start(bf16[98,1024]{1,0:T(8,128)(2,1)} %slice.65), channel_id=1, source_target_pairs={{0,2},{2,4},{4,6},{6,0},{1,3},{3,5},{5,7},{7,1},{8,10},{10,12},{12... | collective-permute-start | bytes 602120 | tf_op jit(solution)/shard_map/ppermute | solution.py:21
  43.3 14.0 %collective-permute-start.6 = (bf16[98,1024]{1,0:T(8,128)(2,1)}, bf16[98,1024]{1,0:T(8,128)(2,1)}, u32[]{:S(2)}, u32[]{:S(2)}) collective-permute-start(bf16[98,1024]{1,0:T(8,128)(2,1)} %slice.66), channel_id=1, source_target_pairs={{0,6},{2,0},{4,2},{6,4},{1,7},{3,1},{5,3},{7,5},{8,14},{10,8},{12,... | collective-permute-start | bytes 602120 | tf_op jit(solution)/shard_map/ppermute | solution.py:21
  50.2 15.0 %collective-permute-start = (bf16[98,2048]{1,0:T(8,128)(2,1)}, bf16[98,2048]{1,0:T(8,128)(2,1)}, u32[]{:S(2)}, u32[]{:S(2)}) collective-permute-start(bf16[98,2048]{1,0:T(8,128)(2,1)} %shard_map.103.refs_1_), channel_id=1, source_target_pairs={{0,1},{1,0},{2,3},{3,2},{4,5},{5,4},{6,7},{7,6},{8,9},{9,8},{10,11... | collective-permute-start | bytes 1204232 | tf_op jit(solution)/shard_map/ppermute | solution.py:21
  52.6 2.8 %copy-start.4 = (bf16[98,2048]{1,0:T(8,128)(2,1)S(1)}, bf16[98,2048]{1,0:T(8,128)(2,1)}, u32[]{:S(2)}) copy-start(bf16[98,2048]{1,0:T(8,128)(2,1)} %copy-done.3) | copy-start | bytes 1204228
  52.9 12.4 %collective-permute-start.2 = (bf16[98,2048]{1,0:T(8,128)(2,1)}, bf16[98,2048]{1,0:T(8,128)(2,1)S(1)}, u32[]{:S(2)}, u32[]{:S(2)}) collective-permute-start(bf16[98,2048]{1,0:T(8,128)(2,1)} %collective-permute-done.1.refs_3_), channel_id=1, source_target_pairs={{0,1},{1,0},{2,3},{3,2},{4,5},{5,4},{6,7},{7,6},{8,9},{9,8},{10,11... | collective-permute-start | bytes 1204232 | tf_op jit(solution)/shard_map/ppermute | solution.py:21
  55.4 9.9 %collective-permute-start.4 = (bf16[98,2048]{1,0:T(8,128)(2,1)S(1)}, bf16[98,2048]{1,0:T(8,128)(2,1)S(1)}, u32[]{:S(2)}, u32[]{:S(2)}) collective-permute-start(bf16[98,2048]{1,0:T(8,128)(2,1)S(1)} %copy-done.4), channel_id=1, source_target_pairs={{0,1},{1,0},{2,3},{3,2},{4,5},{5,4},{6,7},{7,6},{8,9},{9,8},{10,11... | collective-permute-start | bytes 1204232 | tf_op jit(solution)/shard_map/ppermute | solution.py:21
  59.1 6.2 %collective-permute-start.7 = (bf16[98,2048]{1,0:T(8,128)(2,1)}, bf16[98,2048]{1,0:T(8,128)(2,1)S(1)}, u32[]{:S(2)}, u32[]{:S(2)}) collective-permute-start(bf16[98,2048]{1,0:T(8,128)(2,1)} %pad_maximum_fusion), channel_id=1, source_target_pairs={{0,1},{1,0},{2,3},{3,2},{4,5},{5,4},{6,7},{7,6},{8,9},{9,8},{10,11... | collective-permute-start | bytes 1204232 | tf_op jit(solution)/shard_map/ppermute | solution.py:21
  65.3 0.8 copy-start.6
  65.3 0.9 copy-start.7
  74.3 17.2 %collective-permute-start.12 = (bf16[8,256,128]{2,1,0:T(8,128)(2,1)}, bf16[8,256,128]{2,1,0:T(8,128)(2,1)S(1)}, u32[]{:S(2)}, u32[]{:S(2)}) collective-permute-start(bf16[8,256,128]{2,1,0:T(8,128)(2,1)} %get-tuple-element.14), channel_id=1, source_target_pairs={{0,192},{192,384},{384,576},{576,0},{1,193},{193,385},{385,577},{5... | collective-permute-start | bytes 1572872 | tf_op jit(solution)/shard_map/ppermute | solution.py:21
  77.7 26.3 %collective-permute-start.13 = (bf16[8,256,128]{2,1,0:T(8,128)(2,1)}, bf16[8,256,128]{2,1,0:T(8,128)(2,1)S(1)}, u32[]{:S(2)}, u32[]{:S(2)}) collective-permute-start(bf16[8,256,128]{2,1,0:T(8,128)(2,1)} %get-tuple-element.15), channel_id=1, source_target_pairs={{0,576},{192,0},{384,192},{576,384},{1,577},{193,1},{385,193},{577... | collective-permute-start | bytes 1572872 | tf_op jit(solution)/shard_map/ppermute | solution.py:21
  81.3 22.6 %collective-permute-start.14 = (bf16[8,256,128]{2,1,0:T(8,128)(2,1)}, bf16[8,256,128]{2,1,0:T(8,128)(2,1)S(1)}, u32[]{:S(2)}, u32[]{:S(2)}) collective-permute-start(bf16[8,256,128]{2,1,0:T(8,128)(2,1)} %get-tuple-element.16), channel_id=1, source_target_pairs={{0,384},{192,576},{384,0},{576,192},{1,385},{193,577},{385,1},{577... | collective-permute-start | bytes 1572872 | tf_op jit(solution)/shard_map/ppermute | solution.py:21
  106.1 23.6 %all-to-all-start = ((bf16[8,256,128]{2,1,0:T(8,128)(2,1)}), bf16[8,256,128]{2,1,0:T(8,128)(2,1)S(1)}, u32[]{:S(2)}, u32[]{:S(2)}) async-start(bf16[8,256,128]{2,1,0:T(8,128)(2,1)} %add_convert_fusion), calls=%async_computation | async-start | bytes 1048576 | tf_op jit(solution)/shard_map/all_to_all | solution.py:220
  117.1 30.0 %copy-start = (bf16[98,1024]{1,0:T(8,128)(2,1)S(1)}, bf16[98,1024]{1,0:T(8,128)(2,1)}, u32[]{:S(2)}) copy-start(bf16[98,1024]{1,0:T(8,128)(2,1)} %x_ref.1) | copy-start | bytes 602116
  117.1 30.1 %copy-start.5 = (bf16[98,4096]{1,0:T(8,128)(2,1)S(1)}, bf16[98,4096]{1,0:T(8,128)(2,1)}, u32[]{:S(2)}) copy-start(bf16[98,4096]{1,0:T(8,128)(2,1)} %get-tuple-element.11) | copy-start | bytes 2408452
  117.1 30.1 %collective-permute-start.8 = (bf16[98,4096]{1,0:T(8,128)(2,1)}, bf16[98,4096]{1,0:T(8,128)(2,1)S(1)}, u32[]{:S(2)}, u32[]{:S(2)}) collective-permute-start(bf16[98,4096]{1,0:T(8,128)(2,1)} %get-tuple-element.12), channel_id=1, source_target_pairs={{0,1},{1,0},{2,3},{3,2},{4,5},{5,4},{6,7},{7,6},{8,9},{9,8},{10,11... | collective-permute-start | bytes 2408456 | tf_op jit(solution)/shard_map/ppermute | solution.py:21
  130.8 60.6 %copy-start.8 = (f32[1024]{0:T(1024)S(1)}, f32[1024]{0:T(1024)}, u32[]{:S(2)}) copy-start(f32[1024]{0:T(1024)} %param.14) | copy-start | bytes 12292
  130.8 61.8 %all-to-all-start.1 = ((bf16[12,256,128]{2,1,0:T(8,128)(2,1)}), bf16[12,256,128]{2,1,0:T(8,128)(2,1)S(1)}, u32[]{:S(2)}, u32[]{:S(2)}) async-start(bf16[12,256,128]{2,1,0:T(8,128)(2,1)} %broadcast_in_dim.20), calls=%async_computation.1 | async-start | bytes 1572864 | tf_op jit(solution)/shard_map/all_to_all | solution.py:222
  147.2 44.4 %copy-start.1 = (bf16[98,2048]{1,0:T(8,128)(2,1)S(1)}, bf16[98,2048]{1,0:T(8,128)(2,1)}, u32[]{:S(2)}) copy-start(bf16[98,2048]{1,0:T(8,128)(2,1)} %shard_map.103.refs_1_) | copy-start | bytes 1204228
  147.4 33.1 %collective-permute-start.10 = (bf16[98,1024]{1,0:T(8,128)(2,1)S(1)}, bf16[98,1024]{1,0:T(8,128)(2,1)S(1)}, u32[]{:S(2)}, u32[]{:S(2)}) collective-permute-start(bf16[98,1024]{1,0:T(8,128)(2,1)S(1)} %get-tuple-element.24), channel_id=1, source_target_pairs={{0,2},{2,4},{4,6},{6,0},{1,3},{3,5},{5,7},{7,1},{8,10},{10,12},{12... | collective-permute-start | bytes 602120 | tf_op jit(solution)/shard_map/ppermute | solution.py:21
  154.6 30.3 %collective-permute-start.9 = (bf16[98,1024]{1,0:T(8,128)(2,1)S(1)}, bf16[98,1024]{1,0:T(8,128)(2,1)S(1)}, u32[]{:S(2)}, u32[]{:S(2)}) collective-permute-start(bf16[98,1024]{1,0:T(8,128)(2,1)S(1)} %get-tuple-element.23), channel_id=1, source_target_pairs={{0,6},{2,0},{4,2},{6,4},{1,7},{3,1},{5,3},{7,5},{8,14},{10,8},{12,... | collective-permute-start | bytes 602120 | tf_op jit(solution)/shard_map/ppermute | solution.py:21
  180.6 10.7 %collective-permute-start.11 = (bf16[98,1024]{1,0:T(8,128)(2,1)S(1)}, bf16[98,1024]{1,0:T(8,128)(2,1)S(1)}, u32[]{:S(2)}, u32[]{:S(2)}) collective-permute-start(bf16[98,1024]{1,0:T(8,128)(2,1)S(1)} %add_convert_fusion.1), channel_id=1, source_target_pairs={{0,2},{2,4},{4,6},{6,0},{1,3},{3,5},{5,7},{7,1},{8,10},{10,12},{12... | collective-permute-start | bytes 602120 | tf_op jit(solution)/shard_map/ppermute | solution.py:21

commit v3 on v2

--- a/solution.py
+++ b/solution.py
@@ -19,6 +19,16 @@
 def shifted(value, axis, step):
     n = lax.axis_size(axis)
     return lax.ppermute(value, axis, [(i, (i + step) % n) for i in range(n)])
+
+
+def mirrored(value, step):
+    n, nc = lax.axis_size("zh"), lax.axis_size("c")
+    pairs = [
+        (i * nc + c, (i + (step if c == 0 else -step)) % n * nc + c)
+        for i in range(n)
+        for c in range(nc)
+    ]
+    return lax.ppermute(value, ("zh", "c"), pairs)
 
 
 def gelu_pair(hidden_pre):
@@ -174,23 +184,25 @@
     ff = hidden_pre.shape[1]
     padded = -(-rows // 16) * 16
     both_own = norm_and_mask(inputs, grad_out, pad_mask, ln_gain, ln_shift)
-    both3 = shifted(both_own, "zh", 1)
-    both1 = shifted(both_own, "zh", -1)
+    both3 = mirrored(both_own, 1)
+    both1 = mirrored(both_own, -1)
 
     zh, c = lax.axis_index("zh"), lax.axis_index("c")
     h = hidden_pre.reshape(nh, nc, rows, ff)
-    h = lax.dynamic_slice_in_dim(jnp.concatenate([h, h[:-1]], axis=0), zh, nh, axis=0)
+    first = jnp.where(c == 0, zh, nh - 1 - zh)
+    h = jnp.where(c == 0, h, h[::-1])
+    h = lax.dynamic_slice_in_dim(jnp.concatenate([h, h[:-1]], axis=0), first, nh, axis=0)
     h = lax.dynamic_slice_in_dim(jnp.concatenate([h, h[:, :-1]], axis=1), c, nc, axis=1)
     h = jnp.pad(h.reshape(n, rows, ff), ((0, 0), (0, padded - rows), (0, 0)))
     activation, slope = gelu_pair(h.reshape(n * padded, ff))
     act_t = activation.astype(BF).T
 
-    m2 = shifted(both3[:, :d], "zh", 1)
-    n2 = shifted(both1[:, d:], "zh", -1)
+    m2 = mirrored(both3[:, :d], 1)
+    n2 = mirrored(both1[:, d:], -1)
     swaps = []
     for v in (both_own, both3, both1, jnp.concatenate([m2, n2], axis=1)):
         swaps.append(shifted(v, "c", 1))
-    arrays = (both_own, swaps[0], both1, swaps[2], both3, swaps[1], swaps[3], m2, n2)
+    arrays = (both_own, swaps[0], both1, swaps[1], both3, swaps[2], swaps[3], m2, n2)
 
     def spots(k):
         return ((0, k), (1, k), (2, k), (3, k), (7 + k, 0), (6, k), (4, k), (5, k))
@@ -206,12 +218,12 @@
     from_core = shifted(dn_other, "c", 1)
 
     def pair(k):
-        lanes = slice(k * d, (k + 1) * d)
-        return dn_own[:, lanes].astype(F32) + from_core[:, lanes].astype(F32)
-
-    passing = shifted(pair(2).astype(BF), "zh", 1)
-    from_up = shifted(pair(3).astype(BF), "zh", -1)
-    from_down = shifted((pair(1) + passing.astype(F32)).astype(BF), "zh", 1)
+        mine, theirs = (slice(j * d, (j + 1) * d) for j in (k, -k % nh))
+        return dn_own[:, mine].astype(F32) + from_core[:, theirs].astype(F32)
+
+    passing = mirrored(pair(2).astype(BF), 1)
+    from_up = mirrored(pair(3).astype(BF), -1)
+    from_down = mirrored((pair(1) + passing.astype(F32)).astype(BF), 1)
     d_normed = pair(0) + from_up.astype(F32) + from_down.astype(F32)
 
     total = terms[0].astype(F32)

time: 195 us -> 189 us (0.969)
  the two profiles are of different devices: /device:TPU:64 before, /device:TPU:129 now
where the time goes in v3:
time: 189 us; the launch traced here: 188 us
  starting transfers between devices  80.3 us (42%)
  waiting for transfers between devices  76.6 us (41%)
  Pallas kernels  13.9 us (7%)
  other arithmetic  9.45 us (5%)
  local copies, waits for them, and re-layouts  7.09 us (4%)
    ppermute x7, waiting for transfers between devices, mirrored(): return lax.ppermute(value, ('zh', 'c'), pairs)  47.3 us
    ppermute x7, starting transfers between devices, mirrored(): return lax.ppermute(value, ('zh', 'c'), pairs)  35.9 us
    ppermute x8, starting transfers between devices, shifted(): return lax.ppermute(value, axis, [(i, (i + step) % n) for i in range(n)])  32.9 us
    ppermute x8, waiting for transfers between devices, shifted(): return lax.ppermute(value, axis, [(i, (i + step) % n) for i in range(n)])  20.5 us
    pallas_call x2, Pallas kernels, in_hbm(): pl.pallas_call(whole, out_shape=[pltpu.HBM(v.shape, v.dtype) for v in out...  11.8 us
    all_to_all x1, waiting for transfers between devices, shards(): both_y = lax.all_to_all(total.astype(BF), 'y', 0, 0, tiled=True)  8.84 us
    all_to_all x1, starting transfers between devices, shards(): lax.all_to_all(jnp.broadcast_to(both, (nx * nz, *both.shape)), ('x', 'zl'...  6.2 us
    all_to_all x1, starting transfers between devices, shards(): both_y = lax.all_to_all(total.astype(BF), 'y', 0, 0, tiled=True)  5.31 us
  transfers between devices with their start and end apart: 17, of which 8 were waited for; matrix products, arithmetic and copies ran while one was open for 6% of the time, Pallas kernels for 2%

profile of v3, /device:TPU:129, one launch (start us, length us, event | category | flops | bytes accessed | tf_op | source)
XLA Modules:
  0.0 188.4 jit_solution(10651548665504535585)
XLA Ops:
  0.6 2.1 %shard_map.103.refs_1_ = bf16[98,2048]{1,0:T(8,128)(2,1)} custom-call(bf16[98,1024]{1,0:T(8,128)(2,1)} %x_ref.1, bf16[98,1024]{1,0:T(8,128)(2,1)} %g_ref.1, s32[1,98]{1,0:T(1,128)} %bitcast.30, f32[1,1024]{1,0:T(1,128)} %bitcast.28, f32[1,1024]{1,0:T(1,128)} %bitcast.29), custom_call_target="tpu_custom_call" | custom-call | tf_op jit(solution)/shard_map/pallas_call | solution.py:114
  2.7 12.5 %collective-permute-start.2 = (bf16[98,2048]{1,0:T(8,128)(2,1)}, bf16[98,2048]{1,0:T(8,128)(2,1)S(1)}, u32[]{:S(2)}, u32[]{:S(2)}) collective-permute-start(bf16[98,2048]{1,0:T(8,128)(2,1)} %shard_map.103.refs_1_), channel_id=1, source_target_pairs={{0,2},{1,7},{2,4},{3,1},{4,6},{5,3},{6,0},{7,5},{8,10},{9,15},{10,... | collective-permute-start | bytes 1204232 | tf_op jit(solution)/shard_map/ppermute | solution.py:31
  15.2 1.9 %collective-permute-start.1 = (bf16[98,2048]{1,0:T(8,128)(2,1)}, bf16[98,2048]{1,0:T(8,128)(2,1)S(1)}, u32[]{:S(2)}, u32[]{:S(2)}) collective-permute-start(bf16[98,2048]{1,0:T(8,128)(2,1)} %shard_map.103.refs_1_), channel_id=1, source_target_pairs={{0,6},{1,3},{2,0},{3,5},{4,2},{5,7},{6,4},{7,1},{8,14},{9,11},{10,... | collective-permute-start | bytes 1204232 | tf_op jit(solution)/shard_map/ppermute | solution.py:31
  17.1 2.9 %collective-permute-start = (bf16[98,2048]{1,0:T(8,128)(2,1)}, bf16[98,2048]{1,0:T(8,128)(2,1)}, u32[]{:S(2)}, u32[]{:S(2)}) collective-permute-start(bf16[98,2048]{1,0:T(8,128)(2,1)} %shard_map.103.refs_1_), channel_id=1, source_target_pairs={{0,1},{1,0},{2,3},{3,2},{4,5},{5,4},{6,7},{7,6},{8,9},{9,8},{10,11... | collective-permute-start | bytes 1204232 | tf_op jit(solution)/shard_map/ppermute | solution.py:21
  20.0 1.3 reshape.50
  21.4 7.7 %collective-permute-done.2.refs_5_ = bf16[98,2048]{1,0:T(8,128)(2,1)S(1)} collective-permute-done((bf16[98,2048]{1,0:T(8,128)(2,1)}, bf16[98,2048]{1,0:T(8,128)(2,1)S(1)}, u32[]{:S(2)}, u32[]{:S(2)}) %collective-permute-start.2) | collective-permute-done | bytes 401440 | tf_op jit(solution)/shard_map/ppermute | solution.py:31
  29.0 0.8 slice.61
  29.8 7.1 %collective-permute-start.5 = (bf16[98,1024]{1,0:T(8,128)(2,1)}, bf16[98,1024]{1,0:T(8,128)(2,1)S(1)}, u32[]{:S(2)}, u32[]{:S(2)}) collective-permute-start(bf16[98,1024]{1,0:T(8,128)(2,1)} %slice.61), channel_id=1, source_target_pairs={{0,2},{1,7},{2,4},{3,1},{4,6},{5,3},{6,0},{7,5},{8,10},{9,15},{10,... | collective-permute-start | bytes 602120 | tf_op jit(solution)/shard_map/ppermute | solution.py:31
  36.9 7.9 %collective-permute-done.1.refs_3_ = bf16[98,2048]{1,0:T(8,128)(2,1)S(1)} collective-permute-done((bf16[98,2048]{1,0:T(8,128)(2,1)}, bf16[98,2048]{1,0:T(8,128)(2,1)S(1)}, u32[]{:S(2)}, u32[]{:S(2)}) %collective-permute-start.1) | collective-permute-done | bytes 401440 | tf_op jit(solution)/shard_map/ppermute | solution.py:31
  44.9 0.8 slice.62
  45.6 2.4 %collective-permute-start.6 = (bf16[98,1024]{1,0:T(8,128)(2,1)}, bf16[98,1024]{1,0:T(8,128)(2,1)}, u32[]{:S(2)}, u32[]{:S(2)}) collective-permute-start(bf16[98,1024]{1,0:T(8,128)(2,1)} %slice.62), channel_id=1, source_target_pairs={{0,6},{1,3},{2,0},{3,5},{4,2},{5,7},{6,4},{7,1},{8,14},{9,11},{10,... | collective-permute-start | bytes 602120 | tf_op jit(solution)/shard_map/ppermute | solution.py:31
  48.0 0.2 reverse_select_fusion
  48.2 0.3 fusion.9
  48.6 8.4 %collective-permute-start.3 = (bf16[98,2048]{1,0:T(8,128)(2,1)S(1)}, bf16[98,2048]{1,0:T(8,128)(2,1)S(1)}, u32[]{:S(2)}, u32[]{:S(2)}) collective-permute-start(bf16[98,2048]{1,0:T(8,128)(2,1)S(1)} %collective-permute-done.2.refs_5_), channel_id=1, source_target_pairs={{0,1},{1,0},{2,3},{3,2},{4,5},{5,4},{6,7},{7,6},{8,9},{9,8},{10,11... | collective-permute-start | bytes 1204232 | tf_op jit(solution)/shard_map/ppermute | solution.py:21
  56.9 1.9 %collective-permute-start.4 = (bf16[98,2048]{1,0:T(8,128)(2,1)S(1)}, bf16[98,2048]{1,0:T(8,128)(2,1)}, u32[]{:S(2)}, u32[]{:S(2)}) collective-permute-start(bf16[98,2048]{1,0:T(8,128)(2,1)S(1)} %collective-permute-done.1.refs_3_), channel_id=1, source_target_pairs={{0,1},{1,0},{2,3},{3,2},{4,5},{5,4},{6,7},{7,6},{8,9},{9,8},{10,11... | collective-permute-start | bytes 1204232 | tf_op jit(solution)/shard_map/ppermute | solution.py:21
  58.9 1.0 collective-permute-done.6.refs_9_
  59.9 1.7 pad_maximum_fusion
  61.6 7.7 %collective-permute-start.7 = (bf16[98,2048]{1,0:T(8,128)(2,1)}, bf16[98,2048]{1,0:T(8,128)(2,1)S(1)}, u32[]{:S(2)}, u32[]{:S(2)}) collective-permute-start(bf16[98,2048]{1,0:T(8,128)(2,1)} %pad_maximum_fusion), channel_id=1, source_target_pairs={{0,1},{1,0},{2,3},{3,2},{4,5},{5,4},{6,7},{7,6},{8,9},{9,8},{10,11... | collective-permute-start | bytes 1204232 | tf_op jit(solution)/shard_map/ppermute | solution.py:21
  69.3 0.3 fusion.8
  69.7 2.2 %fusion.6 = (f32[896,512]{1,0:T(8,128)}, bf16[512,896]{0,1:T(8,128)(2,1)S(1)}) fusion(bf16[8,112,512]{2,1,0:T(8,128)(2,1)S(1)} %pad.4), kind=kLoop, calls=%fused_computation.11 | loop fusion | flops 5046272 | bytes 3670016 | tf_op jit(solution)/shard_map/add | solution.py:38
  71.9 1.3 copy.16.refs_10_
  73.2 0.8 copy-done.6
  73.9 8.0 %shard_map.104 = (bf16[8,256,128]{2,1,0:T(8,128)(2,1)}, bf16[8,256,128]{2,1,0:T(8,128)(2,1)}, bf16[8,256,128]{2,1,0:T(8,128)(2,1)}, bf16[8,256,128]{2,1,0:T(8,128)(2,1)}, bf16[896,512]{1,0:T(8,128)(2,1)}) custom-call(s32[1]{0:T(128)} %bitcast.3.refs_0_, bf16[98,2048]{1,0:T(8,128)(2,1)} %shard_map.103.refs_1_, bf16[98,2048]{1,0:T(8,128)(2,1)} %collective-permute-done.refs_2_, ...), custom_call_target="tpu_custom_call" | custom-call | tf_op jit(solution)/shard_map/pallas_call | solution.py:65
  81.9 1.9 %collective-permute-start.12 = (bf16[8,256,128]{2,1,0:T(8,128)(2,1)}, bf16[8,256,128]{2,1,0:T(8,128)(2,1)S(1)}, u32[]{:S(2)}, u32[]{:S(2)}) collective-permute-start(bf16[8,256,128]{2,1,0:T(8,128)(2,1)} %get-tuple-element.14), channel_id=1, source_target_pairs={{0,192},{192,384},{384,576},{576,0},{1,193},{193,385},{385,577},{5... | collective-permute-start | bytes 1572872 | tf_op jit(solution)/shard_map/ppermute | solution.py:21
  83.9 4.6 %collective-permute-start.13 = (bf16[8,256,128]{2,1,0:T(8,128)(2,1)}, bf16[8,256,128]{2,1,0:T(8,128)(2,1)S(1)}, u32[]{:S(2)}, u32[]{:S(2)}) collective-permute-start(bf16[8,256,128]{2,1,0:T(8,128)(2,1)} %get-tuple-element.15), channel_id=1, source_target_pairs={{0,576},{192,0},{384,192},{576,384},{1,577},{193,1},{385,193},{577... | collective-permute-start | bytes 1572872 | tf_op jit(solution)/shard_map/ppermute | solution.py:21
  88.4 1.9 %collective-permute-start.14 = (bf16[8,256,128]{2,1,0:T(8,128)(2,1)}, bf16[8,256,128]{2,1,0:T(8,128)(2,1)S(1)}, u32[]{:S(2)}, u32[]{:S(2)}) collective-permute-start(bf16[8,256,128]{2,1,0:T(8,128)(2,1)} %get-tuple-element.16), channel_id=1, source_target_pairs={{0,384},{192,576},{384,0},{576,192},{1,385},{193,577},{385,1},{577... | collective-permute-start | bytes 1572872 | tf_op jit(solution)/shard_map/ppermute | solution.py:21
  90.4 8.9 %collective-permute-done.12 = bf16[8,256,128]{2,1,0:T(8,128)(2,1)S(1)} collective-permute-done((bf16[8,256,128]{2,1,0:T(8,128)(2,1)}, bf16[8,256,128]{2,1,0:T(8,128)(2,1)S(1)}, u32[]{:S(2)}, u32[]{:S(2)}) %collective-permute-start.12) | collective-permute-done | bytes 524320 | tf_op jit(solution)/shard_map/ppermute | solution.py:21
  99.3 11.5 %collective-permute-done.13 = bf16[8,256,128]{2,1,0:T(8,128)(2,1)S(1)} collective-permute-done((bf16[8,256,128]{2,1,0:T(8,128)(2,1)}, bf16[8,256,128]{2,1,0:T(8,128)(2,1)S(1)}, u32[]{:S(2)}, u32[]{:S(2)}) %collective-permute-start.13) | collective-permute-done | bytes 524320 | tf_op jit(solution)/shard_map/ppermute | solution.py:21
  110.8 2.1 %add_convert_fusion = bf16[8,256,128]{2,1,0:T(8,128)(2,1)} fusion(bf16[8,256,128]{2,1,0:T(8,128)(2,1)S(1)} %collective-permute-done.14, bf16[8,256,128]{2,1,0:T(8,128)(2,1)S(1)} %collective-permute-done.13, bf16[8,256,128]{2,1,0:T(8,128)(2,1)S(1)} %collective-permute-done.12, bf16[8,256,128]{2,1,0:T(8,128)(2,1)} %get-tuple-element.13), kind=kLoop, calls=%fused_computation.18 | loop fusion | flops 2097152 | bytes 2621440 | tf_op jit(solution)/shard_map/convert_element_type | solution.py:232
  112.9 5.3 %all-to-all-start = ((bf16[8,256,128]{2,1,0:T(8,128)(2,1)}), bf16[8,256,128]{2,1,0:T(8,128)(2,1)S(1)}, u32[]{:S(2)}, u32[]{:S(2)}) async-start(bf16[8,256,128]{2,1,0:T(8,128)(2,1)} %add_convert_fusion), calls=%async_computation | async-start | bytes 1048576 | tf_op jit(solution)/shard_map/all_to_all | solution.py:232
  118.2 3.9 %shard_map.105 = (bf16[98,4096]{1,0:T(8,128)(2,1)}, bf16[98,4096]{1,0:T(8,128)(2,1)}) custom-call(bf16[896,512]{1,0:T(8,128)(2,1)} %get-tuple-element.10.refs_0_, bf16[1024,512]{1,0:T(8,128)(2,1)} %refs_1_.1), custom_call_target="tpu_custom_call" | custom-call | tf_op jit(solution)/shard_map/pallas_call | solution.py:65
  122.1 3.6 %collective-permute-start.8 = (bf16[98,4096]{1,0:T(8,128)(2,1)}, bf16[98,4096]{1,0:T(8,128)(2,1)S(1)}, u32[]{:S(2)}, u32[]{:S(2)}) collective-permute-start(bf16[98,4096]{1,0:T(8,128)(2,1)} %get-tuple-element.12), channel_id=1, source_target_pairs={{0,1},{1,0},{2,3},{3,2},{4,5},{5,4},{6,7},{7,6},{8,9},{9,8},{10,11... | collective-permute-start | bytes 2408456 | tf_op jit(solution)/shard_map/ppermute | solution.py:21
  125.8 8.8 %all-to-all-done = bf16[8,256,128]{2,1,0:T(8,128)(2,1)S(1)} async-done(((bf16[8,256,128]{2,1,0:T(8,128)(2,1)}), bf16[8,256,128]{2,1,0:T(8,128)(2,1)S(1)}, u32[]{:S(2)}, u32[]{:S(2)}) %all-to-all-start) | async-done | bytes 524320 | tf_op jit(solution)/shard_map/all_to_all | solution.py:232
  134.7 1.0 broadcast_in_dim.20
  135.7 6.2 %all-to-all-start.1 = ((bf16[12,256,128]{2,1,0:T(8,128)(2,1)}), bf16[12,256,128]{2,1,0:T(8,128)(2,1)S(1)}, u32[]{:S(2)}, u32[]{:S(2)}) async-start(bf16[12,256,128]{2,1,0:T(8,128)(2,1)} %broadcast_in_dim.20), calls=%async_computation.1 | async-start | bytes 1572864 | tf_op jit(solution)/shard_map/all_to_all | solution.py:234
  142.1 0.2 add_convert_fusion.3
  142.2 4.9 %collective-permute-start.10 = (bf16[98,1024]{1,0:T(8,128)(2,1)S(1)}, bf16[98,1024]{1,0:T(8,128)(2,1)S(1)}, u32[]{:S(2)}, u32[]{:S(2)}) collective-permute-start(bf16[98,1024]{1,0:T(8,128)(2,1)S(1)} %get-tuple-element.24), channel_id=1, source_target_pairs={{0,2},{1,7},{2,4},{3,1},{4,6},{5,3},{6,0},{7,5},{8,10},{9,15},{10,... | collective-permute-start | bytes 602120 | tf_op jit(solution)/shard_map/ppermute | solution.py:31
  147.2 0.2 fusion.19
  147.4 5.2 %collective-permute-start.9 = (bf16[98,1024]{1,0:T(8,128)(2,1)S(1)}, bf16[98,1024]{1,0:T(8,128)(2,1)S(1)}, u32[]{:S(2)}, u32[]{:S(2)}) collective-permute-start(bf16[98,1024]{1,0:T(8,128)(2,1)S(1)} %get-tuple-element.23), channel_id=1, source_target_pairs={{0,6},{1,3},{2,0},{3,5},{4,2},{5,7},{6,4},{7,1},{8,14},{9,11},{10,... | collective-permute-start | bytes 602120 | tf_op jit(solution)/shard_map/ppermute | solution.py:31
  152.6 23.0 %collective-permute-done.10 = bf16[98,1024]{1,0:T(8,128)(2,1)S(1)} collective-permute-done((bf16[98,1024]{1,0:T(8,128)(2,1)S(1)}, bf16[98,1024]{1,0:T(8,128)(2,1)S(1)}, u32[]{:S(2)}, u32[]{:S(2)}) %collective-permute-start.10) | collective-permute-done | bytes 200736 | tf_op jit(solution)/shard_map/ppermute | solution.py:31
  175.7 1.9 %collective-permute-start.11 = (bf16[98,1024]{1,0:T(8,128)(2,1)S(1)}, bf16[98,1024]{1,0:T(8,128)(2,1)S(1)}, u32[]{:S(2)}, u32[]{:S(2)}) collective-permute-start(bf16[98,1024]{1,0:T(8,128)(2,1)S(1)} %add_convert_fusion.1), channel_id=1, source_target_pairs={{0,2},{1,7},{2,4},{3,1},{4,6},{5,3},{6,0},{7,5},{8,10},{9,15},{10,... | collective-permute-start | bytes 602120 | tf_op jit(solution)/shard_map/ppermute | solution.py:31
  177.7 7.6 %collective-permute-done.11 = bf16[98,1024]{1,0:T(8,128)(2,1)S(1)} collective-permute-done((bf16[98,1024]{1,0:T(8,128)(2,1)S(1)}, bf16[98,1024]{1,0:T(8,128)(2,1)S(1)}, u32[]{:S(2)}, u32[]{:S(2)}) %collective-permute-start.11) | collective-permute-done | bytes 200736 | tf_op jit(solution)/shard_map/ppermute | solution.py:31
  185.3 0.3 fusion.21
  185.6 0.9 fusion.18
  186.5 0.1 convert_reduce_fusion
  186.6 0.8 slice_multiply_fusion
  187.4 0.1 copy.17
  187.5 0.8 copy.18
  (33 shorter events, 0.5 us)
Async XLA Ops:
  2.7 26.3 %collective-permute-start.2 = (bf16[98,2048]{1,0:T(8,128)(2,1)}, bf16[98,2048]{1,0:T(8,128)(2,1)S(1)}, u32[]{:S(2)}, u32[]{:S(2)}) collective-permute-start(bf16[98,2048]{1,0:T(8,128)(2,1)} %shard_map.103.refs_1_), channel_id=1, source_target_pairs={{0,2},{1,7},{2,4},{3,1},{4,6},{5,3},{6,0},{7,5},{8,10},{9,15},{10,... | collective-permute-start | bytes 1204232 | tf_op jit(solution)/shard_map/ppermute | solution.py:31
  15.2 29.7 %collective-permute-start.1 = (bf16[98,2048]{1,0:T(8,128)(2,1)}, bf16[98,2048]{1,0:T(8,128)(2,1)S(1)}, u32[]{:S(2)}, u32[]{:S(2)}) collective-permute-start(bf16[98,2048]{1,0:T(8,128)(2,1)} %shard_map.103.refs_1_), channel_id=1, source_target_pairs={{0,6},{1,3},{2,0},{3,5},{4,2},{5,7},{6,4},{7,1},{8,14},{9,11},{10,... | collective-permute-start | bytes 1204232 | tf_op jit(solution)/shard_map/ppermute | solution.py:31
  17.1 56.0 %collective-permute-start = (bf16[98,2048]{1,0:T(8,128)(2,1)}, bf16[98,2048]{1,0:T(8,128)(2,1)}, u32[]{:S(2)}, u32[]{:S(2)}) collective-permute-start(bf16[98,2048]{1,0:T(8,128)(2,1)} %shard_map.103.refs_1_), channel_id=1, source_target_pairs={{0,1},{1,0},{2,3},{3,2},{4,5},{5,4},{6,7},{7,6},{8,9},{9,8},{10,11... | collective-permute-start | bytes 1204232 | tf_op jit(solution)/shard_map/ppermute | solution.py:21
  29.0 19.5 %copy-start.2 = (bf16[98,2048]{1,0:T(8,128)(2,1)}, bf16[98,2048]{1,0:T(8,128)(2,1)S(1)}, u32[]{:S(2)}) copy-start(bf16[98,2048]{1,0:T(8,128)(2,1)S(1)} %collective-permute-done.2.refs_5_) | copy-start | bytes 1204228
  29.8 29.1 %collective-permute-start.5 = (bf16[98,1024]{1,0:T(8,128)(2,1)}, bf16[98,1024]{1,0:T(8,128)(2,1)S(1)}, u32[]{:S(2)}, u32[]{:S(2)}) collective-permute-start(bf16[98,1024]{1,0:T(8,128)(2,1)} %slice.61), channel_id=1, source_target_pairs={{0,2},{1,7},{2,4},{3,1},{4,6},{5,3},{6,0},{7,5},{8,10},{9,15},{10,... | collective-permute-start | bytes 602120 | tf_op jit(solution)/shard_map/ppermute | solution.py:31
  44.9 12.1 %copy-start.3 = (bf16[98,2048]{1,0:T(8,128)(2,1)}, bf16[98,2048]{1,0:T(8,128)(2,1)S(1)}, u32[]{:S(2)}) copy-start(bf16[98,2048]{1,0:T(8,128)(2,1)S(1)} %collective-permute-done.1.refs_3_) | copy-start | bytes 1204228
  45.6 14.3 %collective-permute-start.6 = (bf16[98,1024]{1,0:T(8,128)(2,1)}, bf16[98,1024]{1,0:T(8,128)(2,1)}, u32[]{:S(2)}, u32[]{:S(2)}) collective-permute-start(bf16[98,1024]{1,0:T(8,128)(2,1)} %slice.62), channel_id=1, source_target_pairs={{0,6},{1,3},{2,0},{3,5},{4,2},{5,7},{6,4},{7,1},{8,14},{9,11},{10,... | collective-permute-start | bytes 602120 | tf_op jit(solution)/shard_map/ppermute | solution.py:31
  48.6 24.6 %collective-permute-start.3 = (bf16[98,2048]{1,0:T(8,128)(2,1)S(1)}, bf16[98,2048]{1,0:T(8,128)(2,1)S(1)}, u32[]{:S(2)}, u32[]{:S(2)}) collective-permute-start(bf16[98,2048]{1,0:T(8,128)(2,1)S(1)} %collective-permute-done.2.refs_5_), channel_id=1, source_target_pairs={{0,1},{1,0},{2,3},{3,2},{4,5},{5,4},{6,7},{7,6},{8,9},{9,8},{10,11... | collective-permute-start | bytes 1204232 | tf_op jit(solution)/shard_map/ppermute | solution.py:21
  56.9 16.2 %collective-permute-start.4 = (bf16[98,2048]{1,0:T(8,128)(2,1)S(1)}, bf16[98,2048]{1,0:T(8,128)(2,1)}, u32[]{:S(2)}, u32[]{:S(2)}) collective-permute-start(bf16[98,2048]{1,0:T(8,128)(2,1)S(1)} %collective-permute-done.1.refs_3_), channel_id=1, source_target_pairs={{0,1},{1,0},{2,3},{3,2},{4,5},{5,4},{6,7},{7,6},{8,9},{9,8},{10,11... | collective-permute-start | bytes 1204232 | tf_op jit(solution)/shard_map/ppermute | solution.py:21
  58.9 10.8 %copy-start.4 = (bf16[98,1024]{1,0:T(8,128)(2,1)}, bf16[98,1024]{1,0:T(8,128)(2,1)S(1)}, u32[]{:S(2)}) copy-start(bf16[98,1024]{1,0:T(8,128)(2,1)S(1)} %collective-permute-done.5.refs_8_) | copy-start | bytes 602116
  61.6 11.5 %collective-permute-start.7 = (bf16[98,2048]{1,0:T(8,128)(2,1)}, bf16[98,2048]{1,0:T(8,128)(2,1)S(1)}, u32[]{:S(2)}, u32[]{:S(2)}) collective-permute-start(bf16[98,2048]{1,0:T(8,128)(2,1)} %pad_maximum_fusion), channel_id=1, source_target_pairs={{0,1},{1,0},{2,3},{3,2},{4,5},{5,4},{6,7},{7,6},{8,9},{9,8},{10,11... | collective-permute-start | bytes 1204232 | tf_op jit(solution)/shard_map/ppermute | solution.py:21
  73.1 0.8 copy-start.6
  81.9 17.4 %collective-permute-start.12 = (bf16[8,256,128]{2,1,0:T(8,128)(2,1)}, bf16[8,256,128]{2,1,0:T(8,128)(2,1)S(1)}, u32[]{:S(2)}, u32[]{:S(2)}) collective-permute-start(bf16[8,256,128]{2,1,0:T(8,128)(2,1)} %get-tuple-element.14), channel_id=1, source_target_pairs={{0,192},{192,384},{384,576},{576,0},{1,193},{193,385},{385,577},{5... | collective-permute-start | bytes 1572872 | tf_op jit(solution)/shard_map/ppermute | solution.py:21
  83.9 27.0 %collective-permute-start.13 = (bf16[8,256,128]{2,1,0:T(8,128)(2,1)}, bf16[8,256,128]{2,1,0:T(8,128)(2,1)S(1)}, u32[]{:S(2)}, u32[]{:S(2)}) collective-permute-start(bf16[8,256,128]{2,1,0:T(8,128)(2,1)} %get-tuple-element.15), channel_id=1, source_target_pairs={{0,576},{192,0},{384,192},{576,384},{1,577},{193,1},{385,193},{577... | collective-permute-start | bytes 1572872 | tf_op jit(solution)/shard_map/ppermute | solution.py:21
  88.4 22.4 %collective-permute-start.14 = (bf16[8,256,128]{2,1,0:T(8,128)(2,1)}, bf16[8,256,128]{2,1,0:T(8,128)(2,1)S(1)}, u32[]{:S(2)}, u32[]{:S(2)}) collective-permute-start(bf16[8,256,128]{2,1,0:T(8,128)(2,1)} %get-tuple-element.16), channel_id=1, source_target_pairs={{0,384},{192,576},{384,0},{576,192},{1,385},{193,577},{385,1},{577... | collective-permute-start | bytes 1572872 | tf_op jit(solution)/shard_map/ppermute | solution.py:21
  112.9 21.7 %all-to-all-start = ((bf16[8,256,128]{2,1,0:T(8,128)(2,1)}), bf16[8,256,128]{2,1,0:T(8,128)(2,1)S(1)}, u32[]{:S(2)}, u32[]{:S(2)}) async-start(bf16[8,256,128]{2,1,0:T(8,128)(2,1)} %add_convert_fusion), calls=%async_computation | async-start | bytes 1048576 | tf_op jit(solution)/shard_map/all_to_all | solution.py:232
  122.1 19.8 %copy-start = (bf16[98,1024]{1,0:T(8,128)(2,1)S(1)}, bf16[98,1024]{1,0:T(8,128)(2,1)}, u32[]{:S(2)}) copy-start(bf16[98,1024]{1,0:T(8,128)(2,1)} %x_ref.1) | copy-start | bytes 602116
  122.1 19.9 %copy-start.5 = (bf16[98,4096]{1,0:T(8,128)(2,1)S(1)}, bf16[98,4096]{1,0:T(8,128)(2,1)}, u32[]{:S(2)}) copy-start(bf16[98,4096]{1,0:T(8,128)(2,1)} %get-tuple-element.11) | copy-start | bytes 2408452
  122.1 19.9 %collective-permute-start.8 = (bf16[98,4096]{1,0:T(8,128)(2,1)}, bf16[98,4096]{1,0:T(8,128)(2,1)S(1)}, u32[]{:S(2)}, u32[]{:S(2)}) collective-permute-start(bf16[98,4096]{1,0:T(8,128)(2,1)} %get-tuple-element.12), channel_id=1, source_target_pairs={{0,1},{1,0},{2,3},{3,2},{4,5},{5,4},{6,7},{7,6},{8,9},{9,8},{10,11... | collective-permute-start | bytes 2408456 | tf_op jit(solution)/shard_map/ppermute | solution.py:21
  135.7 49.6 %copy-start.7 = (f32[1024]{0:T(1024)S(1)}, f32[1024]{0:T(1024)}, u32[]{:S(2)}) copy-start(f32[1024]{0:T(1024)} %param.14) | copy-start | bytes 12292
  135.7 50.8 %all-to-all-start.1 = ((bf16[12,256,128]{2,1,0:T(8,128)(2,1)}), bf16[12,256,128]{2,1,0:T(8,128)(2,1)S(1)}, u32[]{:S(2)}, u32[]{:S(2)}) async-start(bf16[12,256,128]{2,1,0:T(8,128)(2,1)} %broadcast_in_dim.20), calls=%async_computation.1 | async-start | bytes 1572864 | tf_op jit(solution)/shard_map/all_to_all | solution.py:234
  142.1 43.5 %copy-start.1 = (bf16[98,2048]{1,0:T(8,128)(2,1)S(1)}, bf16[98,2048]{1,0:T(8,128)(2,1)}, u32[]{:S(2)}) copy-start(bf16[98,2048]{1,0:T(8,128)(2,1)} %shard_map.103.refs_1_) | copy-start | bytes 1204228
  142.2 33.4 %collective-permute-start.10 = (bf16[98,1024]{1,0:T(8,128)(2,1)S(1)}, bf16[98,1024]{1,0:T(8,128)(2,1)S(1)}, u32[]{:S(2)}, u32[]{:S(2)}) collective-permute-start(bf16[98,1024]{1,0:T(8,128)(2,1)S(1)} %get-tuple-element.24), channel_id=1, source_target_pairs={{0,2},{1,7},{2,4},{3,1},{4,6},{5,3},{6,0},{7,5},{8,10},{9,15},{10,... | collective-permute-start | bytes 602120 | tf_op jit(solution)/shard_map/ppermute | solution.py:31
  147.4 30.3 %collective-permute-start.9 = (bf16[98,1024]{1,0:T(8,128)(2,1)S(1)}, bf16[98,1024]{1,0:T(8,128)(2,1)S(1)}, u32[]{:S(2)}, u32[]{:S(2)}) collective-permute-start(bf16[98,1024]{1,0:T(8,128)(2,1)S(1)} %get-tuple-element.23), channel_id=1, source_target_pairs={{0,6},{1,3},{2,0},{3,5},{4,2},{5,7},{6,4},{7,1},{8,14},{9,11},{10,... | collective-permute-start | bytes 602120 | tf_op jit(solution)/shard_map/ppermute | solution.py:31
  175.7 9.6 %collective-permute-start.11 = (bf16[98,1024]{1,0:T(8,128)(2,1)S(1)}, bf16[98,1024]{1,0:T(8,128)(2,1)S(1)}, u32[]{:S(2)}, u32[]{:S(2)}) collective-permute-start(bf16[98,1024]{1,0:T(8,128)(2,1)S(1)} %add_convert_fusion.1), channel_id=1, source_target_pairs={{0,2},{1,7},{2,4},{3,1},{4,6},{5,3},{6,0},{7,5},{8,10},{9,15},{10,... | collective-permute-start | bytes 602120 | tf_op jit(solution)/shard_map/ppermute | solution.py:31
